TPU v7x, 64 devices: a 2x2x8 block of a 4x4x8 slice. The times are simulated.
64 devices in a mesh: dp: 4 (over x, y), tp: 16 (over z, core).
Axes of the slice: x: 2, y: 2, z: 8, core: 2. Of those that a mesh axis runs over, the one named last changes fastest.
The devices are a block of a 4x4x8 slice.
Arguments:
- x_in: bfloat16 [24, 128, 4096], P('dp', 'tp'), parts along dimension 0
- seg_pos: int32 [24, 128], P('dp'), parts along dimension 0
- conv_state: bfloat16 [2, 24, 3, 4096], P(None, 'dp', None, 'tp'), parts along dimension 1
- lru_state: float32 [2, 24, 4096], P(None, 'dp', 'tp'), parts along dimension 1
- k_cache: bfloat16 [24, 2048, 256], P('dp'), parts along dimension 0
- v_cache: bfloat16 [24, 2048, 256], P('dp'), parts along dimension 0
- slot_pos: int32 [24, 2048], P('dp'), parts along dimension 0
- norm_scale: bfloat16 [6, 4096], replicated
- w_x: bfloat16 [2, 4096, 4096], P(None, None, 'tp')
- b_x: bfloat16 [2, 4096], P(None, 'tp')
- w_y: bfloat16 [2, 4096, 4096], P(None, None, 'tp')
- b_y: bfloat16 [2, 4096], P(None, 'tp')
- conv_w: bfloat16 [2, 4, 4096], P(None, None, 'tp')
- conv_b: bfloat16 [2, 4096], P(None, 'tp')
- w_a: bfloat16 [2, 16, 256, 256], P(None, 'tp')
- b_a: bfloat16 [2, 4096], P(None, 'tp')
- w_i: bfloat16 [2, 16, 256, 256], P(None, 'tp')
- b_i: bfloat16 [2, 4096], P(None, 'tp')
- a_param: float32 [2, 4096], P(None, 'tp')
- w_out: bfloat16 [2, 4096, 4096], P(None, 'tp')
- b_out: bfloat16 [2, 4096], replicated
- w_q: bfloat16 [4096, 4096], P(None, 'tp')
- w_k: bfloat16 [4096, 256], replicated
- w_v: bfloat16 [4096, 256], replicated
- w_o: bfloat16 [4096, 4096], P('tp')
- b_o: bfloat16 [4096], replicated
- w_1: bfloat16 [3, 4096, 12288], P(None, None, 'tp')
- b_1: bfloat16 [3, 12288], P(None, 'tp')
- w_2: bfloat16 [3, 4096, 12288], P(None, None, 'tp')
- b_2: bfloat16 [3, 12288], P(None, 'tp')
- w_d: bfloat16 [3, 12288, 4096], P(None, 'tp')
- b_d: bfloat16 [3, 4096], replicated
Outputs:
- output 1: bfloat16 [24, 128, 4096], P('dp', 'tp'), parts along dimension 0
- output 2: bfloat16 [2, 24, 3, 4096], P(None, 'dp', None, 'tp'), parts along dimension 1
- output 3: float32 [2, 24, 4096], P(None, 'dp', 'tp'), parts along dimension 1
- output 4: bfloat16 [24, 2048, 256], P('dp'), parts along dimension 0
- output 5: bfloat16 [24, 2048, 256], P('dp'), parts along dimension 0
- output 6: int32 [24, 2048], P('dp'), parts along dimension 0
There are 4 independent parts. A program takes and returns all parts, laid end to end along the dimension named above; an argument that names none is the same for every part.
All inputs are finite; a program needn't handle non-finite values.
Results may differ from a plain program's by a relative error of at most 0.02.
Values are sent between devices in bfloat16 or wider.
A program may use at most 768 MiB of HBM per device.

v0:
```python
import jax
import jax.numpy as jnp
from jax import lax
from jax.sharding import PartitionSpec as P

WINDOW = 2048
HEAD_DIM = 256
ROPE_DIM = 128
CONV_WIDTH = 4
SCORE_SCALE = 0.0625
NEG_BIG = -1e30


def rms_norm(hidden, norm_gain):
    hidden_f32 = hidden.astype(jnp.float32)
    inv_rms = lax.rsqrt(jnp.mean(hidden_f32 * hidden_f32, axis=-1, keepdims=True) + 1e-6)
    return (hidden_f32 * inv_rms * (1.0 + norm_gain.astype(jnp.float32))).astype(jnp.bfloat16)


def residual_add(hidden, update, bias_row):
    return (hidden.astype(jnp.float32) + update.astype(jnp.float32) + bias_row.astype(jnp.float32)).astype(jnp.bfloat16)


def linear_map(act_in, weight):
    return jnp.einsum('bcd,df->bcf', act_in, weight, preferred_element_type=jnp.float32)


def apply_rope(proj_f32, pos_exp):
    half_dim = ROPE_DIM // 2
    timescale = 10000.0 ** (2.0 * jnp.arange(half_dim).astype(jnp.float32) / ROPE_DIM)
    angle_rad = pos_exp.astype(jnp.float32) / timescale
    sin_a = jnp.sin(angle_rad)
    cos_a = jnp.cos(angle_rad)
    first_half = proj_f32[..., :half_dim]
    second_half = proj_f32[..., half_dim:ROPE_DIM]
    return jnp.concatenate([first_half * cos_a - second_half * sin_a, second_half * cos_a + first_half * sin_a, proj_f32[..., ROPE_DIM:]], axis=-1).astype(jnp.bfloat16)


def lru_combine(lhs_pair, rhs_pair):
    return lhs_pair[0] * rhs_pair[0], rhs_pair[0] * lhs_pair[1] + rhs_pair[1]


def recurrent_local(normed, is_reset, conv_prev, state_prev, w_x, b_x, w_y, b_y, conv_w, conv_b, w_a, b_a, w_i, b_i, a_param, w_out):
    tok_count = normed.shape[1]
    gate_y = jax.nn.gelu(linear_map(normed, w_y) + b_y.astype(jnp.float32), approximate=True).astype(jnp.bfloat16)
    branch_x = (linear_map(normed, w_x) + b_x.astype(jnp.float32)).astype(jnp.bfloat16)
    padded = jnp.concatenate([conv_prev, branch_x], axis=1)
    conv_f32 = conv_b.astype(jnp.float32) + sum(padded[:, tap_idx:tap_idx + tok_count].astype(jnp.float32) * conv_w[tap_idx].astype(jnp.float32) for tap_idx in range(CONV_WIDTH))
    conv_bf = conv_f32.astype(jnp.bfloat16)
    blocks = conv_bf.reshape(conv_bf.shape[:2] + w_a.shape[:2])
    gate_r = jax.nn.sigmoid(jnp.einsum('bchi,hij->bchj', blocks, w_a, preferred_element_type=jnp.float32).reshape(conv_bf.shape) + b_a.astype(jnp.float32))
    gate_i = jax.nn.sigmoid(jnp.einsum('bchi,hij->bchj', blocks, w_i, preferred_element_type=jnp.float32).reshape(conv_bf.shape) + b_i.astype(jnp.float32))
    decay_a = jnp.exp(-8.0 * gate_r * jax.nn.softplus(a_param))
    multiplier = jnp.where(is_reset, 1.0, jnp.sqrt(1.0 - decay_a * decay_a))
    decay_a = jnp.where(is_reset, 0.0, decay_a)
    is_first = (jnp.arange(tok_count) == 0)[None, :, None]
    drive_in = conv_bf.astype(jnp.float32) * gate_i * multiplier + jnp.where(is_first, decay_a * state_prev[:, None, :], 0.0)
    hidden_seq = lax.associative_scan(lru_combine, (decay_a, drive_in), axis=1)[1]
    mixed_hy = (hidden_seq * gate_y.astype(jnp.float32)).astype(jnp.bfloat16)
    return linear_map(mixed_hy, w_out), branch_x[:, tok_count - (CONV_WIDTH - 1):], hidden_seq[:, tok_count - 1]


def mlp_local(normed, w_1, b_1, w_2, b_2, w_d):
    gate_val = jax.nn.gelu(linear_map(normed, w_1) + b_1.astype(jnp.float32), approximate=True)
    up_val = linear_map(normed, w_2) + b_2.astype(jnp.float32)
    return linear_map((gate_val * up_val).astype(jnp.bfloat16), w_d)


def attention_local(normed, seg_pos, k_cache, v_cache, slot_pos, w_q, w_k, w_v, w_o):
    batch_size, tok_count = seg_pos.shape
    query_rot = apply_rope(linear_map(normed, w_q).reshape(batch_size, tok_count, -1, HEAD_DIM), seg_pos[:, :, None, None])
    key_new = apply_rope(linear_map(normed, w_k), seg_pos[:, :, None])
    value_new = linear_map(normed, w_v).astype(jnp.bfloat16)
    doc_id = jnp.cumsum((seg_pos == 0).astype(jnp.int32), axis=1)
    diff_old = seg_pos[:, :, None] - slot_pos[:, None, :]
    mask_old = (slot_pos[:, None, :] >= 0) & (diff_old >= 0) & (diff_old < WINDOW) & (doc_id[:, :, None] == 0)
    diff_new = seg_pos[:, :, None] - seg_pos[:, None, :]
    mask_new = (diff_new >= 0) & (diff_new < WINDOW) & (doc_id[:, :, None] == doc_id[:, None, :])
    score_old = jnp.where(mask_old[:, None], jnp.einsum('bchd,bwd->bhcw', query_rot, k_cache, preferred_element_type=jnp.float32) * SCORE_SCALE, NEG_BIG)
    score_new = jnp.where(mask_new[:, None], jnp.einsum('cdie,cle->cidl', query_rot, key_new, preferred_element_type=jnp.float32) * SCORE_SCALE, NEG_BIG)
    row_max = jnp.maximum(score_old.max(axis=-1), score_new.max(axis=-1))[..., None]
    exp_old = jnp.exp(score_old - row_max)
    exp_new = jnp.exp(score_new - row_max)
    denom_sum = exp_old.sum(axis=-1, keepdims=True) + exp_new.sum(axis=-1, keepdims=True)
    attn_out = jnp.einsum('bhcw,bwd->bchd', (exp_old / denom_sum).astype(jnp.bfloat16), v_cache, preferred_element_type=jnp.float32) + jnp.einsum('cidl,cle->cdie', (exp_new / denom_sum).astype(jnp.bfloat16), value_new, preferred_element_type=jnp.float32)
    attn_proj = linear_map(attn_out.astype(jnp.bfloat16).reshape(batch_size, tok_count, -1), w_o)
    batch_idx = jnp.arange(batch_size)[:, None]
    slot_new = jnp.mod(seg_pos, WINDOW)
    k_out = k_cache.at[batch_idx, slot_new].set(key_new, unique_indices=True)
    v_out = v_cache.at[batch_idx, slot_new].set(value_new, unique_indices=True)
    slot_out = slot_pos.at[batch_idx, slot_new].set(seg_pos, unique_indices=True)
    return attn_proj, k_out, v_out, slot_out


def gather_tokens(normed_loc):
    return lax.all_gather(normed_loc, 'tp', axis=1, tiled=True)


def scatter_sum(part_f32):
    return lax.psum_scatter(part_f32.astype(jnp.bfloat16), 'tp', scatter_dimension=1, tiled=True)


def solution(mesh):
    def device_body(x_in, seg_pos, conv_state, lru_state, k_cache, v_cache, slot_pos, norm_scale, w_x, b_x, w_y, b_y, conv_w, conv_b, w_a, b_a, w_i, b_i, a_param, w_out, b_out, w_q, w_k, w_v, w_o, b_o, w_1, b_1, w_2, b_2, w_d, b_d):
        is_reset = (seg_pos == 0)[:, :, None]
        hidden = x_in
        conv_list = []
        lru_list = []
        for layer_idx in range(2):
            normed = gather_tokens(rms_norm(hidden, norm_scale[2 * layer_idx]))
            rec_part, conv_new, lru_new = recurrent_local(normed, is_reset, conv_state[layer_idx], lru_state[layer_idx], w_x[layer_idx], b_x[layer_idx], w_y[layer_idx], b_y[layer_idx], conv_w[layer_idx], conv_b[layer_idx], w_a[layer_idx], b_a[layer_idx], w_i[layer_idx], b_i[layer_idx], a_param[layer_idx], w_out[layer_idx])
            hidden = residual_add(hidden, scatter_sum(rec_part), b_out[layer_idx])
            normed = gather_tokens(rms_norm(hidden, norm_scale[2 * layer_idx + 1]))
            mlp_part = mlp_local(normed, w_1[layer_idx], b_1[layer_idx], w_2[layer_idx], b_2[layer_idx], w_d[layer_idx])
            hidden = residual_add(hidden, scatter_sum(mlp_part), b_d[layer_idx])
            conv_list.append(conv_new)
            lru_list.append(lru_new)
        normed = gather_tokens(rms_norm(hidden, norm_scale[4]))
        attn_part, k_out, v_out, slot_out = attention_local(normed, seg_pos, k_cache, v_cache, slot_pos, w_q, w_k, w_v, w_o)
        hidden = residual_add(hidden, scatter_sum(attn_part), b_o)
        normed = gather_tokens(rms_norm(hidden, norm_scale[5]))
        mlp_part = mlp_local(normed, w_1[2], b_1[2], w_2[2], b_2[2], w_d[2])
        hidden = residual_add(hidden, scatter_sum(mlp_part), b_d[2])
        return hidden, jnp.stack(conv_list), jnp.stack(lru_list), k_out, v_out, slot_out

    col_spec = P(None, None, 'tp')
    vec_spec = P(None, 'tp')
    block_spec = P(None, 'tp', None, None)
    row_spec = P(None, 'tp', None)
    cache_spec = P('dp', None, None)
    arg_specs = (P('dp', 'tp', None), P('dp', None), P(None, 'dp', None, 'tp'), P(None, 'dp', 'tp'), cache_spec, cache_spec, P('dp', None), P(), col_spec, vec_spec, col_spec, vec_spec, col_spec, vec_spec, block_spec, vec_spec, block_spec, vec_spec, vec_spec, row_spec, P(), P(None, 'tp'), P(), P(), P('tp', None), P(), col_spec, vec_spec, col_spec, vec_spec, row_spec, P())
    result_specs = (P('dp', 'tp', None), P(None, 'dp', None, 'tp'), P(None, 'dp', 'tp'), cache_spec, cache_spec, P('dp', None))
    return jax.shard_map(device_body, mesh=mesh, in_specs=arg_specs, out_specs=result_specs, check_vma=False)
```

profile of v0, /device:TPU:21, one launch (start us, length us, event | category | flops | bytes accessed | tf_op | source)
XLA Modules:
  0.0 1114.5 jit_solution(12079145020611085286)
XLA Ops:
  8.3 6.4 copy.116
  24.9 42.6 %all-gather.7.cloned.1.call-done = bf16[6,128,4096]{2,1,0:T(8,128)(2,1)} async-done(((bf16[6,8,4096]{2,1,0:T(8,128)(2,1)}), bf16[6,128,4096]{2,1,0:T(8,128)(2,1)}) %all-gather.7.cloned.1.call-update) | async-done | bytes 6291472 | tf_op jit(solution)/shard_map/all_gather | solution.py:96
  67.5 5.3 fusion.134
  107.2 14.0 %fusion.321 = bf16[16,8,6,4096]{3,1,0,2:T(8,128)(2,1)} fusion(bf16[2,256,4096]{2,1,0:T(8,128)(2,1)} %param.51, bf16[6,128,4096]{2,1,0:T(8,128)(2,1)} %all-gather.7.cloned.1.call-done, bf16[2,4096,256]{2,1,0:T(8,128)(2,1)} %param.42, f32[6,128,256]{2,1,0:T(8,128)} %pad.98, f32[6,128,256]{2,1,0:T(8,128)S(1)} %pad.99, f32[256]{0:T(256)} %bitcast.411), kind=kOutput, calls=%fused_computation.441 | convolution fusion | flops 3227123712 | bytes 18351104 | tf_op jit(solution)/shard_map/bcd,df->bcf/dot_general | solution.py:25
  121.2 6.2 copy.79
  128.8 57.7 %reduce-scatter.19.cloned.1.call-done = bf16[8,24576]{1,0:T(8,128)(2,1)} async-done(((bf16[128,24576]{1,0:T(8,128)(2,1)}), bf16[8,24576]{1,0:T(8,128)(2,1)}) %reduce-scatter.19.cloned.1.call-update) | async-done | bytes 393232
  190.4 44.5 %all-gather.9.cloned.1.call-done = bf16[6,128,4096]{2,1,0:T(8,128)(2,1)} async-done(((bf16[6,8,4096]{2,1,0:T(8,128)(2,1)}), bf16[6,128,4096]{2,1,0:T(8,128)(2,1)}) %all-gather.9.cloned.1.call-update) | async-done | bytes 6291472 | tf_op jit(solution)/shard_map/all_gather | solution.py:96
  234.9 10.0 fusion.11
  244.9 21.2 %fusion.312 = bf16[16,8,6,4096]{3,1,0,2:T(8,128)(2,1)} fusion(bf16[3,768,4096]{2,1,0:T(8,128)(2,1)} %param.62, f32[6,128,768]{2,1,0:T(8,128)} %fusion.11, bf16[6,128,4096]{2,1,0:T(8,128)(2,1)} %all-gather.9.cloned.1.call-done, bf16[3,4096,768]{2,1,0:T(8,128)(2,1)} %param.58, f32[768]{0:T(1024)S(1)} %get-tuple-element.28, f32[768]{0:T(1024)S(1)} %get-tuple-element.118), kind=kOutput, calls=%fused_computation.438 | convolution fusion | flops 9673900032 | bytes 27531264 | tf_op jit(solution)/shard_map/bcd,df->bcf/dot_general | solution.py:25
  266.0 6.2 copy.80
  273.6 57.7 %reduce-scatter.21.cloned.1.call-done = bf16[8,24576]{1,0:T(8,128)(2,1)} async-done(((bf16[128,24576]{1,0:T(8,128)(2,1)}), bf16[8,24576]{1,0:T(8,128)(2,1)}) %reduce-scatter.21.cloned.1.call-update) | async-done | bytes 393232
  336.9 44.6 %all-gather.11.cloned.1.call-done = bf16[6,128,4096]{2,1,0:T(8,128)(2,1)} async-done(((bf16[6,8,4096]{2,1,0:T(8,128)(2,1)}), bf16[6,128,4096]{2,1,0:T(8,128)(2,1)}) %all-gather.11.cloned.1.call-update) | async-done | bytes 6291472 | tf_op jit(solution)/shard_map/all_gather | solution.py:96
  381.6 5.3 fusion.131
  421.5 14.0 %fusion.326 = bf16[16,8,6,4096]{3,1,0,2:T(8,128)(2,1)} fusion(bf16[2,256,4096]{2,1,0:T(8,128)(2,1)} %param.51, bf16[6,128,4096]{2,1,0:T(8,128)(2,1)} %all-gather.11.cloned.1.call-done, bf16[2,4096,256]{2,1,0:T(8,128)(2,1)} %param.42, f32[6,128,256]{2,1,0:T(8,128)} %pad.112, f32[6,128,256]{2,1,0:T(8,128)S(1)} %pad.113, f32[256]{0:T(256)} %bitcast.407), kind=kOutput, calls=%fused_computation.442 | convolution fusion | flops 3227123712 | bytes 18351104 | tf_op jit(solution)/shard_map/bcd,df->bcf/dot_general | solution.py:25
  435.5 6.2 copy.81
  442.0 58.7 %reduce-scatter.23.cloned.1.call-done = bf16[8,24576]{1,0:T(8,128)(2,1)} async-done(((bf16[128,24576]{1,0:T(8,128)(2,1)}), bf16[8,24576]{1,0:T(8,128)(2,1)}) %reduce-scatter.23.cloned.1.call-update) | async-done | bytes 393232
  505.8 45.1 %all-gather.13.cloned.1.call-done = bf16[6,128,4096]{2,1,0:T(8,128)(2,1)} async-done(((bf16[6,8,4096]{2,1,0:T(8,128)(2,1)}), bf16[6,128,4096]{2,1,0:T(8,128)(2,1)}) %all-gather.13.cloned.1.call-update) | async-done | bytes 6291472 | tf_op jit(solution)/shard_map/all_gather | solution.py:96
  551.0 10.0 fusion.6
  561.0 21.2 %fusion.315 = bf16[16,8,6,4096]{3,1,0,2:T(8,128)(2,1)} fusion(bf16[3,768,4096]{2,1,0:T(8,128)(2,1)} %param.62, f32[6,128,768]{2,1,0:T(8,128)} %fusion.6, bf16[6,128,4096]{2,1,0:T(8,128)(2,1)} %all-gather.13.cloned.1.call-done, bf16[3,4096,768]{2,1,0:T(8,128)(2,1)} %param.58, f32[768]{0:T(1024)S(1)} %copy-done.47, f32[768]{0:T(1024)S(1)} %copy-done.48), kind=kOutput, calls=%fused_computation.439 | convolution fusion | flops 9673900032 | bytes 27531264 | tf_op jit(solution)/shard_map/bcd,df->bcf/dot_general | solution.py:25
  582.2 6.2 copy.82
  588.5 58.9 %reduce-scatter.25.cloned.1.call-done = bf16[8,24576]{1,0:T(8,128)(2,1)} async-done(((bf16[128,24576]{1,0:T(8,128)(2,1)}), bf16[8,24576]{1,0:T(8,128)(2,1)}) %reduce-scatter.25.cloned.1.call-update) | async-done | bytes 393232
  651.2 44.6 %all-gather.15.cloned.1.call-done = bf16[6,128,4096]{2,1,0:T(8,128)(2,1)} async-done(((bf16[6,8,4096]{2,1,0:T(8,128)(2,1)}), bf16[6,128,4096]{2,1,0:T(8,128)(2,1)}) %all-gather.15.cloned.1.call-update) | async-done | bytes 6291472 | tf_op jit(solution)/shard_map/all_gather | solution.py:96
  695.8 5.3 fusion.87
  724.8 6.3 copy.83
  731.8 58.4 %reduce-scatter.27.cloned.1.call-done = bf16[8,24576]{1,0:T(8,128)(2,1)} async-done(((bf16[128,24576]{1,0:T(8,128)(2,1)}), bf16[8,24576]{1,0:T(8,128)(2,1)}) %reduce-scatter.27.cloned.1.call-update) | async-done | bytes 393232
  793.7 44.9 %all-gather.17.cloned.1.call-done = bf16[6,128,4096]{2,1,0:T(8,128)(2,1)} async-done(((bf16[6,8,4096]{2,1,0:T(8,128)(2,1)}), bf16[6,128,4096]{2,1,0:T(8,128)(2,1)}) %all-gather.17.cloned.1.call-update) | async-done | bytes 6291472 | tf_op jit(solution)/shard_map/all_gather | solution.py:96
  838.6 10.0 fusion.1
  848.6 21.2 %fusion.318 = bf16[16,8,6,4096]{3,1,0,2:T(8,128)(2,1)} fusion(bf16[3,768,4096]{2,1,0:T(8,128)(2,1)} %param.62, f32[6,128,768]{2,1,0:T(8,128)} %fusion.1, bf16[6,128,4096]{2,1,0:T(8,128)(2,1)} %all-gather.17.cloned.1.call-done, bf16[3,4096,768]{2,1,0:T(8,128)(2,1)} %param.58, f32[768]{0:T(1024)S(1)} %copy-done.45, f32[768]{0:T(1024)S(1)} %copy-done.46), kind=kOutput, calls=%fused_computation.440 | convolution fusion | flops 9673900032 | bytes 27531264 | tf_op jit(solution)/shard_map/bcd,df->bcf/dot_general | solution.py:25
  869.8 6.2 copy.84
  880.5 94.1 %scatter_fusion = bf16[6,2048,256]{2,1,0:T(8,128)(2,1)} fusion(bf16[6,2048,256]{2,1,0:T(8,128)(2,1)} %copy.116, s32[768]{0:T(1024)S(1)} %fusion.273, bf16[768,256]{1,0:T(8,128)(2,1)} %bitcast.358), kind=kCustom, calls=%fused_computation | custom fusion | bytes 1185792 | tf_op jit(solution)/shard_map/scatter | solution.py:89
  974.6 35.9 %scatter_fusion.2 = s32[6,2048]{1,0:T(8,128)S(1)} fusion(s32[6,2048]{1,0:T(8,128)S(1)} %copy.118, s32[768]{0:T(1024)S(1)} %fusion.273, s32[768]{0:T(1024)S(1)} %bitcast.379), kind=kCustom, calls=%fused_computation.2 | custom fusion | bytes 15360 | tf_op jit(solution)/shard_map/scatter | solution.py:91
  1010.5 94.0 %scatter_fusion.1 = bf16[6,2048,256]{2,1,0:T(8,128)(2,1)} fusion(bf16[6,2048,256]{2,1,0:T(8,128)(2,1)} %copy.117, s32[768]{0:T(1024)S(1)} %fusion.273, bf16[768,256]{1,0:T(8,128)(2,1)S(1)} %bitcast.357), kind=kCustom, calls=%fused_computation.1 | custom fusion | bytes 1185792 | tf_op jit(solution)/shard_map/scatter | solution.py:90
  (406 shorter events, 135.4 us)
Async XLA Ops:
  7.2 712.5 %copy-start = (bf16[256,4096]{1,0:T(8,128)(2,1)S(1)}, bf16[256,4096]{1,0:T(8,128)(2,1)}, u32[]{:S(2)}) copy-start(bf16[256,4096]{1,0:T(8,128)(2,1)} %param.56) | copy-start | bytes 6291460
  7.2 60.3 %all-gather.7.cloned.1.call-start = ((), (), s32[]{:S(2)}) async-start(), calls=%async_computation.6 | async-start | bytes 6684672 | tf_op jit(solution)/shard_map/all_gather | solution.py:96
  19.4 167.1 %reduce-scatter.19.cloned.1.call-start = ((), (), s32[]{:S(2)}) async-start(), calls=%async_computation.12 | async-start | bytes 6684672
  127.4 61.2 %copy-start.23 = (f32[1,4096]{1,0:T(1,128)S(1)}, f32[1,4096]{1,0:T(1,128)}, u32[]{:S(2)}) copy-start(f32[1,4096]{1,0:T(1,128)} %get-tuple-element.61) | copy-start | bytes 49156
  127.4 62.3 %copy-start.30 = (bf16[3,768]{1,0:T(4,128)(2,1)S(1)}, bf16[3,768]{1,0:T(4,128)(2,1)}, u32[]{:S(2)}) copy-start(bf16[3,768]{1,0:T(4,128)(2,1)} %param.61) | copy-start | bytes 13828
  127.4 62.3 %copy-start.31 = (bf16[3,768]{1,0:T(4,128)(2,1)S(1)}, bf16[3,768]{1,0:T(4,128)(2,1)}, u32[]{:S(2)}) copy-start(bf16[3,768]{1,0:T(4,128)(2,1)} %param.59) | copy-start | bytes 13828
  127.5 107.4 %all-gather.9.cloned.1.call-start = ((), (), s32[]{:S(2)}) async-start(), calls=%async_computation.7 | async-start | bytes 6684672 | tf_op jit(solution)/shard_map/all_gather | solution.py:96
  189.6 141.7 %reduce-scatter.21.cloned.1.call-start = ((), (), s32[]{:S(2)}) async-start(), calls=%async_computation.13 | async-start | bytes 6684672
  272.2 63.1 %copy-start.22 = (f32[1,4096]{1,0:T(1,128)S(1)}, f32[1,4096]{1,0:T(1,128)}, u32[]{:S(2)}) copy-start(f32[1,4096]{1,0:T(1,128)} %get-tuple-element.60) | copy-start | bytes 49156
  272.2 64.6 %copy-start.28 = (f32[1,6,256]{2,0,1:T(1,128)S(1)}, f32[1,6,256]{2,0,1:T(1,128)}, u32[]{:S(2)}) copy-start(f32[1,6,256]{2,0,1:T(1,128)} %get-tuple-element.85) | copy-start | bytes 18436
  272.2 64.6 %copy-start.17 = (bf16[1,6,3,256]{3,0,2,1:T(2,128)(2,1)S(1)}, bf16[1,6,3,256]{3,0,2,1:T(2,128)(2,1)}, u32[]{:S(2)}) copy-start(bf16[1,6,3,256]{3,0,2,1:T(2,128)(2,1)} %get-tuple-element.79) | copy-start | bytes 27652
  272.2 64.7 %copy-start.44 = (f32[1,256]{1,0:T(1,128)S(1)}, f32[1,256]{1,0:T(1,128)}, u32[]{:S(2)}) copy-start(f32[1,256]{1,0:T(1,128)} %get-tuple-element.97) | copy-start | bytes 3076
  272.3 109.3 %copy-start.54 = (f32[1,256]{1,0:T(1,128)S(1)}, f32[1,256]{1,0:T(1,128)}, u32[]{:S(2)}) copy-start(f32[1,256]{1,0:T(1,128)} %get-tuple-element.107) | copy-start | bytes 3076
  272.3 109.2 %all-gather.11.cloned.1.call-start = ((), (), s32[]{:S(2)}) async-start(), calls=%async_computation.8 | async-start | bytes 6684672 | tf_op jit(solution)/shard_map/all_gather | solution.py:96
  336.3 164.4 %reduce-scatter.23.cloned.1.call-start = ((), (), s32[]{:S(2)}) async-start(), calls=%async_computation.14 | async-start | bytes 6684672
  441.7 61.5 %copy-start.26 = (f32[1,4096]{1,0:T(1,128)S(1)}, f32[1,4096]{1,0:T(1,128)}, u32[]{:S(2)}) copy-start(f32[1,4096]{1,0:T(1,128)} %get-tuple-element.82) | copy-start | bytes 49156
  441.7 63.1 %copy-start.21 = (f32[1,4096]{1,0:T(1,128)S(1)}, f32[1,4096]{1,0:T(1,128)}, u32[]{:S(2)}) copy-start(f32[1,4096]{1,0:T(1,128)} %get-tuple-element.59) | copy-start | bytes 49156
  441.7 109.2 %all-gather.13.cloned.1.call-start = ((), (), s32[]{:S(2)}) async-start(), calls=%async_computation.9 | async-start | bytes 6684672 | tf_op jit(solution)/shard_map/all_gather | solution.py:96
  505.7 55.2 %copy-start.47 = (f32[768]{0:T(1024)S(1)}, f32[768]{0:T(1024)}, u32[]{:S(2)}) copy-start(f32[768]{0:T(1024)} %get-tuple-element.29) | copy-start | bytes 9220
  505.7 55.2 %copy-start.48 = (f32[768]{0:T(1024)S(1)}, f32[768]{0:T(1024)}, u32[]{:S(2)}) copy-start(f32[768]{0:T(1024)} %get-tuple-element.117) | copy-start | bytes 9220
  505.8 141.6 %reduce-scatter.25.cloned.1.call-start = ((), (), s32[]{:S(2)}) async-start(), calls=%async_computation.15 | async-start | bytes 6684672
  588.4 60.6 %copy-start.27 = (f32[1,4096]{1,0:T(1,128)S(1)}, f32[1,4096]{1,0:T(1,128)}, u32[]{:S(2)}) copy-start(f32[1,4096]{1,0:T(1,128)} %get-tuple-element.70) | copy-start | bytes 49156
  588.4 61.2 %copy-start.20 = (f32[1,4096]{1,0:T(1,128)S(1)}, f32[1,4096]{1,0:T(1,128)}, u32[]{:S(2)}) copy-start(f32[1,4096]{1,0:T(1,128)} %get-tuple-element.63) | copy-start | bytes 49156
  588.4 107.4 %all-gather.15.cloned.1.call-start = ((), (), s32[]{:S(2)}) async-start(), calls=%async_computation.10 | async-start | bytes 6684672 | tf_op jit(solution)/shard_map/all_gather | solution.py:96
  650.6 139.6 %reduce-scatter.27.cloned.1.call-start = ((), (), s32[]{:S(2)}) async-start(), calls=%async_computation.16 | async-start | bytes 6684672
  731.1 61.3 %copy-start.19 = (f32[1,4096]{1,0:T(1,128)S(1)}, f32[1,4096]{1,0:T(1,128)}, u32[]{:S(2)}) copy-start(f32[1,4096]{1,0:T(1,128)} %get-tuple-element.58) | copy-start | bytes 49156
  731.2 107.4 %all-gather.17.cloned.1.call-start = ((), (), s32[]{:S(2)}) async-start(), calls=%async_computation.11 | async-start | bytes 6684672 | tf_op jit(solution)/shard_map/all_gather | solution.py:96
  793.4 55.2 %copy-start.45 = (f32[768]{0:T(1024)S(1)}, f32[768]{0:T(1024)}, u32[]{:S(2)}) copy-start(f32[768]{0:T(1024)} %get-tuple-element.27) | copy-start | bytes 9220
  793.4 311.2 %reduce-scatter.29.cloned.1.call-start = ((), (), s32[]{:S(2)}) async-start(), calls=%async_computation.17 | async-start | bytes 6684672
  880.5 130.0 %copy-start.4 = (bf16[6,128,256]{2,1,0:T(8,128)(2,1)S(1)}, bf16[6,128,256]{2,1,0:T(8,128)(2,1)}, u32[]{:S(2)}) copy-start(bf16[6,128,256]{2,1,0:T(8,128)(2,1)} %copy-done.3) | copy-start | bytes 1179652
  974.6 131.6 %copy-start.25 = (f32[1,4096]{1,0:T(1,128)S(1)}, f32[1,4096]{1,0:T(1,128)}, u32[]{:S(2)}) copy-start(f32[1,4096]{1,0:T(1,128)} %get-tuple-element.68) | copy-start | bytes 49156
  1010.5 96.7 %copy-start.1 = (s32[6,2048]{1,0:T(8,128)}, s32[6,2048]{1,0:T(8,128)S(1)}, u32[]{:S(2)}) copy-start(s32[6,2048]{1,0:T(8,128)S(1)} %scatter_fusion.2) | copy-start | bytes 147460
  (51 other events, 674.3 us)
Sparse Core Ops, SparseCore 0:
  19.5 47.9 all-gather.6
  127.6 58.7 reduce-scatter.18
  189.8 45.0 all-gather.8
  272.5 58.7 reduce-scatter.20
  336.4 45.0 all-gather.10
  441.9 58.7 reduce-scatter.22
  505.9 45.0 all-gather.12
  588.6 58.7 reduce-scatter.24
  650.7 45.0 all-gather.14
  731.3 58.8 reduce-scatter.26
  793.5 45.0 all-gather.16
  876.2 58.7 reduce-scatter.28
where the time goes:
time: 1130 us; the launch traced here: 1110 us
  waiting for transfers between devices  558 us (49%)
  local copies, waits for them, and re-layouts  338 us (30%)
  matrix products  159 us (14%)
  other arithmetic  40.5 us (4%)
  between operations  16.2 us (1%)
    unnamed x18, waiting for transfers between devices  292 us
    all_gather x6, waiting for transfers between devices, gather_tokens(): return lax.all_gather(normed_loc, 'tp', axis=1, tiled=True)  266 us
    dot_general x14, matrix products, linear_map(): jnp.einsum('bcd,df->bcf', act_in, weight, preferred_element_type=jnp.floa...  148 us
    scatter x1, local copies, waits for them, and re-layouts, attention_local(): k_out = k_cache.at[batch_idx, slot_new].set(key_new, unique_indices=True)  94.1 us
    scatter x1, local copies, waits for them, and re-layouts, attention_local(): v_out = v_cache.at[batch_idx, slot_new].set(value_new, unique_indices=True)  94 us
    unnamed x162, local copies, waits for them, and re-layouts  61.7 us
    slice x78, local copies, waits for them, and re-layouts, recurrent_local(): lax.associative_scan(lru_combine, (decay_a, drive_in), axis=1)[1]  36 us
    scatter x1, local copies, waits for them, and re-layouts, attention_local(): slot_pos.at[batch_idx, slot_new].set(seg_pos, unique_indices=True)  35.9 us
  transfers between devices with their start and end apart: 12, of which 11 were waited for; matrix products, arithmetic and copies ran while one was open for 21% of the time, Pallas kernels for 0%

commit v1 on v0

v1 whole, which is shorter than its diff:
```python
import functools

import jax
import jax.numpy as jnp
from jax import lax
from jax.experimental import pallas as pl
from jax.experimental.pallas import tpu as pltpu
from jax.sharding import PartitionSpec as P

WINDOW = 2048
HEAD_DIM = 256
ROPE_DIM = 128
CONV_WIDTH = 4
SCORE_SCALE = 0.0625
NEG_BIG = -1e30
F32 = jnp.float32
BF16 = jnp.bfloat16

SLOT_REL = (0, -1, 1, -2, 2, -3, 3, 4)
NC = 4
HALF = NC // 2
UP_ORDER = (0, 1, 2, 3)
DOWN_ORDER = (2, 3, 0, 1)


def slot_of(rel):
    if rel == 0:
        return 0
    if rel in (4, -4):
        return 7
    return -2 * rel - 1 if rel < 0 else 2 * rel


class Net:
    def __init__(self, tp, rows, dim, g, pown, dsend, drecv, zsend, zrecv, ag_z, ag_d, rs_z, rs_d, send_z, send_d):
        self.me = lax.axis_index('tp')
        self.core = lax.rem(self.me, 2)
        self.chips = tp // 2
        self.chip = lax.div(self.me, 2)
        self.up = lax.rem(self.me + 2, tp)
        self.down = lax.rem(self.me + tp - 2, tp)
        self.partner = self.me + 1 - 2 * self.core
        self.rows = rows
        self.dim = dim
        self.cw = dim // NC
        self.g, self.pown, self.dsend, self.drecv, self.zsend, self.zrecv = g, pown, dsend, drecv, zsend, zrecv
        self.ag_z, self.ag_d, self.rs_z, self.rs_d, self.send_z, self.send_d = ag_z, ag_d, rs_z, rs_d, send_z, send_d

    def barrier(self):
        sem = pltpu.get_barrier_semaphore()
        for other in (self.up, self.down, self.partner):
            pl.semaphore_signal(sem, inc=1, device_id={'tp': other}, device_id_type=pl.DeviceIdType.MESH)
        pl.semaphore_wait(sem, 3)

    def cols(self, ch):
        return pl.ds(ch * self.cw, self.cw)

    def remote(self, src, dst, send, recv, dev):
        return pltpu.make_async_remote_copy(src_ref=src, dst_ref=dst, send_sem=send, recv_sem=recv, device_id={'tp': dev}, device_id_type=pl.DeviceIdType.MESH)

    def ag_hop(self, way, d, ch):
        sign = -1 if way == 0 else 1
        src, dst = slot_of(sign * (d - 1)), slot_of(sign * d)
        return self.remote(self.g.at[2 * src + self.core, :, self.cols(ch)], self.g.at[2 * dst + self.core, :, self.cols(ch)],
                           self.send_z.at[way, d - 1, ch], self.ag_z.at[way, d - 1, ch], self.up if way == 0 else self.down)

    def ag_pair(self, slot, ch):
        ref = self.g.at[2 * slot + self.core, :, self.cols(ch)]
        return self.remote(ref, ref, self.send_d.at[slot, ch], self.ag_d.at[slot, ch], self.partner)

    def rs_pair(self, slot, ch):
        return self.remote(self.dsend.at[slot, :, self.cols(ch)], self.drecv.at[slot, :, self.cols(ch)],
                           self.send_d.at[slot, ch], self.rs_d.at[slot, ch], self.partner)

    def rs_hop(self, way, d, ch):
        return self.remote(self.zsend.at[way, d - 1, :, self.cols(ch)], self.zrecv.at[way, d - 1, :, self.cols(ch)],
                           self.send_z.at[way, d - 1, ch], self.rs_z.at[way, d - 1, ch], self.up if way == 0 else self.down)

    def last_hop(self, way, ch):
        return ch < HALF if way == 0 else ch >= HALF

    def hops(self):
        for way in range(2):
            for d in range(1, 5):
                for ch in range(NC):
                    if d < 4 or self.last_hop(way, ch):
                        yield way, d, ch

    def abs_chip(self, rel):
        return lax.rem(self.chip + (rel + self.chips), self.chips)

    def wait_pair(self, slots):
        for slot in slots:
            for ch in range(NC):
                self.ag_pair(slot, ch).wait_recv()

    def gather(self, run_pass):
        for p in range(NC):
            self.ag_hop(0, 1, UP_ORDER[p]).start()
            self.ag_hop(1, 1, DOWN_ORDER[p]).start()
        for ch in range(NC):
            self.ag_pair(0, ch).start()
        self.wait_pair((0,))
        run_pass(0, 1)
        for d in range(1, 5):
            for p in range(NC if d < 4 else HALF):
                for way, order in ((0, UP_ORDER), (1, DOWN_ORDER)):
                    ch = order[p]
                    self.ag_hop(way, d, ch).wait_recv()
                    if d < 3 or (d == 3 and self.last_hop(way, ch)):
                        self.ag_hop(way, d + 1, ch).start()
                    self.ag_pair(slot_of(-d if way == 0 else d), ch).start()
                if p == 0 and d > 1:
                    self.wait_pair((2 * d - 3, 2 * d - 2))
                    run_pass(2 * d - 3, 2 * d - 1)
        self.wait_pair((7,))
        run_pass(7, 8)
        for way, d, ch in self.hops():
            self.ag_hop(way, d, ch).wait_send()
        for slot in range(8):
            for ch in range(NC):
                self.ag_pair(slot, ch).wait_send()

    def reduce(self, lhs_of, w_ref, finish):
        rows = self.rows
        sub = min(512, self.cw)

        def slots_of(d):
            return {4: (7,), 0: (0,)}.get(d, (slot_of(-d), slot_of(d)))

        def compute(d, ch):
            slots = slots_of(d)
            lhs = jnp.concatenate([lhs_of(s, self.core) for s in slots] + [lhs_of(s, 1 - self.core) for s in slots], axis=0)
            for t in range(self.cw // sub):
                span = pl.ds(ch * self.cw + t * sub, sub)
                out = jnp.dot(lhs, w_ref[:, span], preferred_element_type=F32)
                for i, s in enumerate(slots):
                    self.pown[s, :, span] = out[i * rows:(i + 1) * rows]
                    self.dsend[s, :, span] = out[(len(slots) + i) * rows:(len(slots) + i + 1) * rows].astype(BF16)
            for s in slots:
                self.rs_pair(s, ch).start()

        def combine(way, d, ch):
            s = slot_of(d if way == 0 else -d)
            self.rs_pair(s, ch).wait_recv()
            total = self.pown[s, :, self.cols(ch)] + self.drecv[s, :, self.cols(ch)].astype(F32)
            if d < 3 or (d == 3 and self.last_hop(way, ch)):
                self.rs_hop(way, d + 1, ch).wait_recv()
                total = total + self.zrecv[way, d, :, self.cols(ch)].astype(F32)
            self.zsend[way, d - 1, :, self.cols(ch)] = total.astype(BF16)
            self.rs_hop(way, d, ch).start()

        order = tuple(x for i in range(HALF) for x in (i, i + HALF))
        for ch in order:
            compute(4, ch)
        for ch in order[:HALF]:
            compute(3, ch)
        for p in range(HALF):
            combine(0, 4, p)
            combine(1, 4, HALF + p)
        for ch in order[HALF:]:
            compute(3, ch)
        for d in (3, 2, 1):
            for p in range(NC):
                combine(0, d, (p + HALF) % NC)
                combine(1, d, p)
                compute(d - 1, order[p])
        for ch in range(NC):
            self.rs_pair(0, ch).wait_recv()
            self.rs_hop(0, 1, ch).wait_recv()
            self.rs_hop(1, 1, ch).wait_recv()
            total = self.pown[0, :, self.cols(ch)] + self.drecv[0, :, self.cols(ch)].astype(F32)
            total = total + self.zrecv[0, 0, :, self.cols(ch)].astype(F32) + self.zrecv[1, 0, :, self.cols(ch)].astype(F32)
            finish(self.cols(ch), total)
        for way, d, ch in self.hops():
            self.rs_hop(way, d, ch).wait_send()
        for slot in range(8):
            for ch in range(NC):
                self.rs_pair(slot, ch).wait_send()


def comm_kernel(cfg, names, outs, scratch, *refs):
    r = dict(zip(names + outs + scratch, refs))
    x_ref = r['x']
    rows, dim = x_ref.shape
    net = Net(cfg['tp'], rows, dim, r['g'], r.get('pown'), r.get('dsend'), r.get('drecv'), r.get('zsend'), r.get('zrecv'),
              r['ag_z'], r['ag_d'], r['rs_z'], r['rs_d'], r['send_z'], r['send_d'])
    loads = {}
    for i, (key, src, layer) in enumerate(cfg['loads']):
        view = r[src] if layer is None else r[src].at[layer]
        loads[key] = pltpu.make_async_copy(view, r[key], r['w_sem'].at[i])
        loads[key].start()
    net.barrier()
    xbuf = r['xbuf']
    xbuf[...] = x_ref[...]
    eps = 1e-6

    def normalize(idx):
        gain = 1.0 + r['norm'][idx:idx + 1, :].astype(F32)

        def body(i, carry):
            span = pl.ds(pl.multiple_of(i * 16, 16), 16)
            h = xbuf[span, :].astype(F32)
            inv = lax.rsqrt(jnp.mean(h * h, axis=-1, keepdims=True) + eps)
            r['g'][net.core, span, :] = (h * inv * gain).astype(BF16)
            return carry
        lax.fori_loop(0, rows // 16, body, 0)

    def finish_with(bias_ref, idx):
        def finish(cols, total):
            bias = bias_ref[idx:idx + 1, cols].astype(F32)
            xbuf[:, cols] = (xbuf[:, cols].astype(F32) + total + bias).astype(BF16)
        return finish

    def block_of(first, last):
        return r['g'][2 * first:2 * last].reshape((last - first) * 2 * rows, dim)

    if cfg['pre'] is not None:
        r['apre'][...] = r['mid'][...].astype(BF16)
        loads['w_pre'].wait()

        def lhs_pre(slot, core):
            blk = 2 * net.abs_chip(SLOT_REL[slot]) + core
            return r['apre'][pl.ds(pl.multiple_of(blk * rows, 16), rows), :]
        net.reduce(lhs_pre, r['w_pre'], finish_with(r['b_pre'], cfg['pre']))

    if cfg['mlp'] is not None:
        m = cfg['mlp']
        normalize(2 * m + 1)
        pending = ['w_1s', 'w_2s']

        def mlp_pass(first, last):
            while pending:
                loads[pending.pop()].wait()
            count = 2 * (last - first)
            ff = r['w_1s'].shape[1]

            def body(t, carry):
                cols = pl.ds(pl.multiple_of(t * 256, 256), 256)
                lhs = block_of(first, last)
                h1 = jnp.dot(lhs, r['w_1s'][:, cols], preferred_element_type=F32) + r['b_1'][m:m + 1, cols].astype(F32)
                h2 = jnp.dot(lhs, r['w_2s'][:, cols], preferred_element_type=F32) + r['b_2'][m:m + 1, cols].astype(F32)
                act = (jax.nn.gelu(h1, approximate=True) * h2).astype(BF16)
                r['act'][2 * first:2 * last, :, cols] = act.reshape(count, rows, 256)
                return carry
            lax.fori_loop(0, ff // 256, body, 0)
        net.gather(mlp_pass)
        loads['w_ds'].wait()
        net.reduce(lambda slot, core: r['act'][2 * slot + core], r['w_ds'], finish_with(r['b_d'], m))

    if cfg['post'] is not None:
        kind, idx = cfg['post']
        normalize(4 if kind == 'attn' else 2 * idx)
        waiting = [key for key, _, _ in cfg['loads'] if key.startswith('p_')]

        def post_pass(first, last):
            while waiting:
                loads[waiting.pop()].wait()
            lhs = block_of(first, last)
            spans = [pl.ds(pl.multiple_of(net.abs_chip(SLOT_REL[s]) * 2 * rows, 16), 2 * rows) for s in range(first, last)]

            def put(ref, value, rope=False):
                for i, span in enumerate(spans):
                    v = value[i * 2 * rows:(i + 1) * 2 * rows]
                    if rope:
                        lo = v[:, :ROPE_DIM]
                        lo = lo * r['cos'][span, :] + pltpu.roll(lo, ROPE_DIM // 2, 1) * r['sin'][span, :]
                        v = jnp.concatenate([lo, v[:, ROPE_DIM:]], axis=1)
                    ref[span, :] = v.astype(BF16).astype(F32)
            if kind == 'rec':
                put(r['o_u'], jnp.dot(lhs, r['p_x'][...], preferred_element_type=F32) + r['b_x'][idx:idx + 1, :].astype(F32))
                put(r['o_y'], jax.nn.gelu(jnp.dot(lhs, r['p_y'][...], preferred_element_type=F32) + r['b_y'][idx:idx + 1, :].astype(F32), approximate=True))
            else:
                put(r['o_q'], jnp.dot(lhs, r['p_q'][...], preferred_element_type=F32), True)
                put(r['o_k'], jnp.dot(lhs, r['p_k'][...], preferred_element_type=F32), True)
                put(r['o_v'], jnp.dot(lhs, r['p_v'][...], preferred_element_type=F32))
        net.gather(post_pass)
    if 'o_x' in r:
        r['o_x'][...] = xbuf[...]


def comm_call(tp, ident, x, pre=None, mlp=None, post=None):
    rows, dim = x.shape
    vmem, hbm = pl.BlockSpec(memory_space=pltpu.VMEM), pl.BlockSpec(memory_space=pl.ANY)
    args, specs, names, loads, scratch = [], [], [], [], {}

    def add(name, value, spec):
        names.append(name)
        args.append(value)
        specs.append(spec)
    add('x', x, vmem)
    outs = {}
    flops = 0
    if pre is not None or mlp is not None:
        outs['o_x'] = jax.ShapeDtypeStruct((rows, dim), BF16)
        scratch['pown'] = pltpu.VMEM((8, rows, dim), F32)
        scratch['dsend'] = pltpu.VMEM((8, rows, dim), BF16)
        scratch['drecv'] = pltpu.VMEM((8, rows, dim), BF16)
        scratch['zsend'] = pltpu.VMEM((2, 4, rows, dim), BF16)
        scratch['zrecv'] = pltpu.VMEM((2, 4, rows, dim), BF16)
    if pre is not None:
        mid, b_idx, w_pre, layer, b_pre = pre
        add('mid', mid, vmem)
        add('h_pre', w_pre, hbm)
        add('b_pre', b_pre, vmem)
        loads.append(('w_pre', 'h_pre', layer))
        scratch['w_pre'] = pltpu.VMEM(w_pre.shape[-2:], BF16)
        scratch['apre'] = pltpu.VMEM(mid.shape, BF16)
        flops += 2 * mid.shape[0] * w_pre.shape[-2] * dim
    if mlp is not None:
        m, norm, w_1, b_1, w_2, b_2, w_d, b_d = mlp
        ff = w_1.shape[-1]
        for key, value in (('h_1', w_1), ('h_2', w_2), ('h_d', w_d)):
            add(key, value, hbm)
        for key, value in (('b_1', b_1), ('b_2', b_2), ('b_d', b_d)):
            add(key, value, vmem)
        loads += [('w_1s', 'h_1', m), ('w_2s', 'h_2', m), ('w_ds', 'h_d', m)]
        scratch['w_1s'] = pltpu.VMEM((dim, ff), BF16)
        scratch['w_2s'] = pltpu.VMEM((dim, ff), BF16)
        scratch['w_ds'] = pltpu.VMEM((ff, dim), BF16)
        scratch['act'] = pltpu.VMEM((tp, rows, ff), BF16)
        flops += 6 * tp * rows * ff * dim
    else:
        norm = post[2]
    add('norm', norm, vmem)
    if post is not None:
        kind, idx, _, weights, extras = post
        width = weights[0][1].shape[-1]
        for key, value, layer in weights:
            add('h_' + key, value, hbm)
            loads.append((key, 'h_' + key, layer))
            scratch[key] = pltpu.VMEM(value.shape[-2:], BF16)
            outs['o_' + key[2:] if kind == 'attn' else {'p_x': 'o_u', 'p_y': 'o_y'}[key]] = jax.ShapeDtypeStruct((tp * rows, width), F32)
            flops += 2 * tp * rows * dim * width
        for key, value in extras:
            add(key, value, vmem)
    scratch['g'] = pltpu.VMEM((tp, rows, dim), BF16)
    scratch['xbuf'] = pltpu.VMEM((rows, dim), BF16)
    for key in ('ag_z', 'rs_z', 'send_z'):
        scratch[key] = pltpu.SemaphoreType.DMA((2, 4, NC))
    for key in ('ag_d', 'rs_d', 'send_d'):
        scratch[key] = pltpu.SemaphoreType.DMA((8, NC))
    scratch['w_sem'] = pltpu.SemaphoreType.DMA((len(loads),))
    cfg = dict(tp=tp, loads=tuple(loads), pre=None if pre is None else pre[1], mlp=None if mlp is None else mlp[0],
               post=None if post is None else (post[0], post[1]))
    result = pl.pallas_call(
        functools.partial(comm_kernel, cfg, names, list(outs), list(scratch)),
        out_shape=tuple(outs.values()),
        in_specs=specs,
        out_specs=tuple(vmem for _ in outs),
        scratch_shapes=list(scratch.values()),
        compiler_params=pltpu.CompilerParams(collective_id=ident, has_side_effects=True, vmem_limit_bytes=66 * 1000 * 1000),
        cost_estimate=pl.CostEstimate(flops=flops, bytes_accessed=flops // 1500, transcendentals=0),
        name='ring_' + str(ident),
    )(*args)
    return dict(zip(outs, result))


def rec_kernel(layer, seqs, u_ref, y_ref, pos_ref, cs_ref, ls_ref, cw_ref, cb_ref, wa_ref, ba_ref, wi_ref, bi_ref, sp_ref, hy_ref, co_ref, lo_ref, pad):
    blocks = u_ref.shape[0]
    toks = blocks * 8
    width = u_ref.shape[-1]

    def one_seq(s, carry):
        u = u_ref[:, s].reshape(toks, width)
        pad[8:8 + toks, :] = u
        pad[5:8, :] = cs_ref[s].astype(F32)
        co_ref[s] = u[toks - 3:, :].astype(BF16)
        total = jnp.zeros((toks, width), F32)
        for j in range(CONV_WIDTH):
            total = total + pad[5 + j:5 + j + toks, :] * cw_ref[layer, j:j + 1, :].astype(F32)
        conv = (total + cb_ref[layer:layer + 1, :].astype(F32)).astype(BF16)
        gate_r = jax.nn.sigmoid(jnp.dot(conv, wa_ref[0], preferred_element_type=F32) + ba_ref[layer:layer + 1, :].astype(F32))
        gate_i = jax.nn.sigmoid(jnp.dot(conv, wi_ref[0], preferred_element_type=F32) + bi_ref[layer:layer + 1, :].astype(F32))
        decay = jnp.exp(-8.0 * gate_r * sp_ref[layer:layer + 1, :])
        reset = pos_ref[s] == 0
        mult = jnp.where(reset, 1.0, jnp.sqrt(1.0 - decay * decay))
        decay = jnp.where(reset, 0.0, decay)
        drive = conv.astype(F32) * gate_i * mult
        a = decay.reshape(blocks, 8, width)
        b = drive.reshape(blocks, 8, width)
        row = lax.broadcasted_iota(jnp.int32, (blocks, 8, width), 1)
        for k in (1, 2, 4):
            inside = row >= k
            a_sh = jnp.where(inside, pltpu.roll(a, k, 1), 1.0)
            b_sh = jnp.where(inside, pltpu.roll(b, k, 1), 0.0)
            b = a * b_sh + b
            a = a * a_sh
        state = ls_ref[pl.ds(s, 1), :]
        for blk in range(blocks):
            h = a[blk] * state + b[blk]
            state = h[7:8, :]
            hy_ref[blk, s] = (h * y_ref[blk, s]).astype(BF16).astype(F32)
        lo_ref[pl.ds(s, 1), :] = state
        return carry
    lax.fori_loop(0, seqs, one_seq, 0)


def rec_call(layer, u, y, pos_col, conv_state, lru_state, conv_w, conv_b, w_a, b_a, w_i, b_i, soft):
    seqs = pos_col.shape[0]
    toks = pos_col.shape[1]
    width = u.shape[-1]
    blocks = toks // 8
    shape4 = (blocks, seqs, 8, width)
    full = pl.BlockSpec(memory_space=pltpu.VMEM)
    layer_spec = lambda a: pl.BlockSpec((None,) + a.shape[1:], functools.partial(lambda n, i: (layer,) + (0,) * n, a.ndim - 1))
    whole = lambda a: pl.BlockSpec(a.shape, functools.partial(lambda n, i: (0,) * n, a.ndim))
    out_shape = (jax.ShapeDtypeStruct(shape4, F32), jax.ShapeDtypeStruct((seqs, 3, width), BF16), jax.ShapeDtypeStruct((seqs, width), F32))
    args = (u.reshape(shape4), y.reshape(shape4), pos_col, conv_state, lru_state, conv_w, conv_b, w_a, b_a, w_i, b_i, soft)
    per_layer = {3, 4, 7, 9}
    return pl.pallas_call(
        functools.partial(rec_kernel, layer, seqs),
        grid=(1,),
        out_shape=out_shape,
        in_specs=[layer_spec(a) if i in per_layer else whole(a) for i, a in enumerate(args)],
        out_specs=tuple(whole(a) for a in out_shape),
        scratch_shapes=[pltpu.VMEM((toks + 8, width), F32)],
        cost_estimate=pl.CostEstimate(flops=4 * toks * seqs * width * width, bytes_accessed=16 * toks * seqs * width, transcendentals=0),
        name='recurrence_' + str(layer),
    )(*args)


def attn_kernel(q_ref, k_ref, v_ref, kc_ref, vc_ref, slot_ref, pos_row_ref, pos_col_ref, doc_row_ref, doc_col_ref, o_ref, ko_ref, vo_ref, so_ref):
    blocks, _, _, width = q_ref.shape
    toks = blocks * 8
    q = q_ref[...].reshape(toks, width).astype(BF16)
    kn = k_ref[...].reshape(toks, width).astype(BF16)
    vn = v_ref[...].reshape(toks, width).astype(BF16)
    kc, vc = kc_ref[0], vc_ref[0]
    slot = slot_ref[0]
    pos_row, pos_col, doc_row, doc_col = pos_row_ref[0], pos_col_ref[0], doc_row_ref[0], doc_col_ref[0]
    contract = (((1,), (1,)), ((), ()))
    diff_old = pos_col - slot
    keep_old = (slot >= 0) & (diff_old >= 0) & (diff_old < WINDOW) & (doc_col == 0)
    diff_new = pos_col - pos_row
    keep_new = (diff_new >= 0) & (diff_new < WINDOW) & (doc_col == doc_row)
    s_old = jnp.where(keep_old, lax.dot_general(q, kc, contract, preferred_element_type=F32) * SCORE_SCALE, NEG_BIG)
    s_new = jnp.where(keep_new, lax.dot_general(q, kn, contract, preferred_element_type=F32) * SCORE_SCALE, NEG_BIG)
    top = jnp.maximum(jnp.max(s_old, axis=-1, keepdims=True), jnp.max(s_new, axis=-1, keepdims=True))
    e_old = jnp.exp(s_old - top)
    e_new = jnp.exp(s_new - top)
    denom = jnp.sum(e_old, axis=-1, keepdims=True) + jnp.sum(e_new, axis=-1, keepdims=True)
    inv = 1.0 / denom
    out = jnp.dot((e_old * inv).astype(BF16), vc, preferred_element_type=F32) + jnp.dot((e_new * inv).astype(BF16), vn, preferred_element_type=F32)
    o_ref[...] = out.astype(BF16).astype(F32).reshape(o_ref.shape)
    window = kc.shape[0]
    target_row = lax.rem(pos_row, window)
    target_col = lax.rem(pos_col, window)
    hit = lax.broadcasted_iota(jnp.int32, (window, toks), 0) == target_row
    pick = jnp.where(hit, 1.0, 0.0)
    any_hit = jnp.max(pick, axis=1, keepdims=True) > 0.0
    pick = pick.astype(BF16)
    ko_ref[0] = jnp.where(any_hit, jnp.dot(pick, kn, preferred_element_type=F32), kc.astype(F32)).astype(BF16)
    vo_ref[0] = jnp.where(any_hit, jnp.dot(pick, vn, preferred_element_type=F32), vc.astype(F32)).astype(BF16)
    hit_t = lax.broadcasted_iota(jnp.int32, (toks, window), 1) == target_col
    newest = jnp.max(jnp.where(hit_t, pos_col, -1), axis=0, keepdims=True)
    so_ref[0] = jnp.where(newest >= 0, newest, slot)


def attn_call(q, k, v, k_cache, v_cache, slot_pos, seg_pos):
    seqs, toks = seg_pos.shape
    width = q.shape[-1]
    blocks = toks // 8
    window = k_cache.shape[1]
    shape4 = (blocks, seqs, 8, width)
    doc = jnp.cumsum((seg_pos == 0).astype(jnp.int32), axis=1)
    tok_spec = pl.BlockSpec((blocks, 1, 8, width), lambda s: (0, s, 0, 0))
    cache_spec = pl.BlockSpec((1, window, width), lambda s: (s, 0, 0))
    row_spec = lambda n: pl.BlockSpec((1, 1, n), lambda s: (s, 0, 0))
    col_spec = pl.BlockSpec((1, toks, 1), lambda s: (s, 0, 0))
    out, k_out, v_out, slot_out = pl.pallas_call(
        attn_kernel,
        grid=(seqs,),
        out_shape=(jax.ShapeDtypeStruct(shape4, F32), jax.ShapeDtypeStruct(k_cache.shape, BF16), jax.ShapeDtypeStruct(v_cache.shape, BF16), jax.ShapeDtypeStruct((seqs, 1, window), jnp.int32)),
        in_specs=[tok_spec, tok_spec, tok_spec, cache_spec, cache_spec, row_spec(window), row_spec(toks), col_spec, row_spec(toks), col_spec],
        out_specs=(tok_spec, cache_spec, cache_spec, row_spec(window)),
        cost_estimate=pl.CostEstimate(flops=8 * seqs * toks * window * width, bytes_accessed=8 * seqs * window * width, transcendentals=0),
        name='attention',
    )(q.reshape(shape4), k.reshape(shape4), v.reshape(shape4), k_cache, v_cache, slot_pos[:, None, :], seg_pos[:, None, :], seg_pos[:, :, None], doc[:, None, :], doc[:, :, None])
    return out.reshape(blocks * seqs * 8, width), k_out, v_out, slot_out.reshape(slot_pos.shape)


def solution(mesh):
    tp = mesh.shape['tp']

    def device_body(x_in, seg_pos, conv_state, lru_state, k_cache, v_cache, slot_pos, norm_scale, w_x, b_x, w_y, b_y, conv_w, conv_b, w_a, b_a, w_i, b_i, a_param, w_out, b_out, w_q, w_k, w_v, w_o, b_o, w_1, b_1, w_2, b_2, w_d, b_d):
        seqs, toks = seg_pos.shape
        dim = x_in.shape[-1]
        x = x_in.reshape(-1, dim)
        pos_col = seg_pos[:, :, None]
        soft = jax.nn.softplus(a_param)
        half = ROPE_DIM // 2
        timescale = 10000.0 ** (2.0 * jnp.arange(half).astype(F32) / ROPE_DIM)
        order = seg_pos.reshape(seqs, toks // 8, 8).swapaxes(0, 1).reshape(-1)
        angle = order[:, None].astype(F32) / timescale
        sin, cos = jnp.sin(angle), jnp.cos(angle)
        cos2 = jnp.concatenate([cos, cos], axis=1)
        sin2 = jnp.concatenate([-sin, sin], axis=1)

        def rec_post(layer):
            return ('rec', layer, norm_scale, (('p_x', w_x, layer), ('p_y', w_y, layer)), (('b_x', b_x), ('b_y', b_y)))

        def mlp_part(m):
            return (m, norm_scale, w_1, b_1, w_2, b_2, w_d, b_d)

        conv_list, lru_list = [], []
        out = comm_call(tp, 0, x, post=rec_post(0))
        for layer in range(2):
            mid, conv_new, lru_new = rec_call(layer, out['o_u'], out['o_y'], pos_col, conv_state, lru_state, conv_w, conv_b, w_a, b_a, w_i, b_i, soft)
            conv_list.append(conv_new)
            lru_list.append(lru_new)
            post = rec_post(1) if layer == 0 else ('attn', 0, norm_scale, (('p_q', w_q, None), ('p_k', w_k, None), ('p_v', w_v, None)), (('cos', cos2), ('sin', sin2)))
            out = comm_call(tp, layer + 1, x, pre=(mid.reshape(tp * x.shape[0], -1), layer, w_out, layer, b_out), mlp=mlp_part(layer), post=post)
            x = out['o_x']
        mid, k_out, v_out, slot_out = attn_call(out['o_q'], out['o_k'], out['o_v'], k_cache, v_cache, slot_pos, seg_pos)
        out = comm_call(tp, 3, x, pre=(mid, 0, w_o, None, b_o[None, :]), mlp=mlp_part(2))
        return out['o_x'].reshape(x_in.shape), jnp.stack(conv_list), jnp.stack(lru_list), k_out, v_out, slot_out

    col_spec = P(None, None, 'tp')
    vec_spec = P(None, 'tp')
    block_spec = P(None, 'tp', None, None)
    row_spec = P(None, 'tp', None)
    cache_spec = P('dp', None, None)
    arg_specs = (P('dp', 'tp', None), P('dp', None), P(None, 'dp', None, 'tp'), P(None, 'dp', 'tp'), cache_spec, cache_spec, P('dp', None), P(), col_spec, vec_spec, col_spec, vec_spec, col_spec, vec_spec, block_spec, vec_spec, block_spec, vec_spec, vec_spec, row_spec, P(), P(None, 'tp'), P(), P(), P('tp', None), P(), col_spec, vec_spec, col_spec, vec_spec, row_spec, P())
    result_specs = (P('dp', 'tp', None), P(None, 'dp', None, 'tp'), P(None, 'dp', 'tp'), cache_spec, cache_spec, P('dp', None))
    return jax.shard_map(device_body, mesh=mesh, in_specs=arg_specs, out_specs=result_specs, check_vma=False)
```

time: 1130 us -> 504 us (0.45)
  waiting for transfers between devices: 558 us -> 0 us
  Pallas kernels: 0 us -> 481 us
  local copies, waits for them, and re-layouts: 338 us -> 9.44 us
  matrix products: 159 us -> 0 us
  other arithmetic: 40.5 us -> 3.54 us
  between operations: 16.2 us -> 1.04 us
    pallas_call x0 -> x7, Pallas kernels: none -> 481 us  [the longest x4 454 us: comm_call(): pl.pallas_call(functools.partial(comm_kernel, cfg, names, list(outs), lis...]
    unnamed x18 -> x0, waiting for transfers between devices: 292 us -> none
    all_gather x6 -> x0, waiting for transfers between devices: 266 us -> none  [gather_tokens(): return lax.all_gather(normed_loc, 'tp', axis=1, tiled=True)]
    scatter x3 -> x0, local copies, waits for them, and re-layouts: 224 us -> none  [the longest x1 94.1 us: attention_local(): k_out = k_cache.at[batch_idx, slot_new].set(key_new, unique_indices=True)]
    dot_general x21 -> x0, matrix products: 159 us -> none  [the longest x14 148 us: linear_map(): jnp.einsum('bcd,df->bcf', act_in, weight, preferred_element_type=jnp.floa...]
    unnamed x162 -> x28, local copies, waits for them, and re-layouts: 61.7 us -> 4.91 us
    slice x82 -> x0, local copies, waits for them, and re-layouts: 37.9 us -> none  [the longest x78 36 us: recurrent_local(): lax.associative_scan(lru_combine, (decay_a, drive_in), axis=1)[1]]
    pad x24 -> x0, local copies, waits for them, and re-layouts: 12.8 us -> none  [recurrent_local(): lax.associative_scan(lru_combine, (decay_a, drive_in), axis=1)[1]]
  transfers between devices with their start and end apart: 12 -> 0, of which waited for: 11 -> 0; matrix products, arithmetic and copies ran while one was open for 21% -> 0% of each run, Pallas kernels for 0% -> 0%
where the time goes in v1:
time: 504 us; the launch traced here: 495 us
  Pallas kernels  481 us (95%)
  local copies, waits for them, and re-layouts  9.44 us (2%)
    pallas_call x4, Pallas kernels, comm_call(): pl.pallas_call(functools.partial(comm_kernel, cfg, names, list(outs), lis...  454 us
    pallas_call x1, Pallas kernels, attn_call(): pl.pallas_call(attn_kernel, grid=(seqs,), out_shape=(jax.ShapeDtypeStruct...  16 us
    pallas_call x2, Pallas kernels, rec_call(): pl.pallas_call(functools.partial(rec_kernel, layer, seqs), grid=(1,), out...  10.3 us

profile of v1, /device:TPU:21, one launch (start us, length us, event | category | flops | bytes accessed | tf_op | source)
XLA Modules:
  0.0 494.6 jit_solution(17092232285693188607)
XLA Ops:
  0.6 0.0 copy-start
  0.6 0.0 copy-start.3
  0.7 0.0 copy-start.4
  0.7 0.0 copy-start.10
  0.7 45.9 %ring_0.1 = (f32[768,256]{1,0:T(8,128)}, f32[768,256]{1,0:T(8,128)}) custom-call(bf16[48,4096]{1,0:T(8,128)(2,1)} %bitcast.41, bf16[6,4096]{1,0:T(8,128)(2,1)} %refs_10_.5, bf16[2,4096,256]{2,1,0:T(8,128)(2,1)} %refs_11_.2, bf16[2,4096,256]{2,1,0:T(8,128)(2,1)} %refs_12_.2, bf16[2,256]{1,0:T(2,128)(2,1)} %refs_13_.2, bf16[2,256]{1,0:T(2,128)(2,1)} %refs_14_.1), custom_call_target="tpu_custom_call" | custom-call | flops 3221225472 | bytes 2147483 | tf_op jit(solution)/shard_map/ring_0/pallas_call | solution.py:346
  46.6 0.0 copy-done
  46.6 0.9 copy.44.pos_ref.pos_col_ref
  47.6 0.0 copy-done.3
  47.6 0.6 copy.45.cs_ref
  48.2 0.6 copy.46.ls_ref
  48.8 0.6 compare_select_fusion.sp_ref
  49.4 5.1 %recurrence_0.1 = (f32[16,6,8,256]{3,2,1,0:T(8,128)}, bf16[6,3,256]{2,1,0:T(4,128)(2,1)}, f32[6,256]{1,0:T(8,128)}) custom-call(f32[16,6,8,256]{3,2,1,0:T(8,128)} %bitcast.29, f32[16,6,8,256]{3,2,1,0:T(8,128)} %bitcast.30, s32[6,128,1]{2,1,0:T(8,128)} %copy.44.pos_ref.pos_col_ref, bf16[2,6,3,256]{3,2,1,0:T(4,128)(2,1)} %copy.45.cs_ref, ...), custom_call_target="tpu_custom_call" | custom-call | flops 201326592 | bytes 3145728 | tf_op jit(solution)/shard_map/recurrence_0/pallas_call | solution.py:411
  54.5 147.7 %ring_1.1 = (bf16[48,4096]{1,0:T(8,128)(2,1)}, f32[768,256]{1,0:T(8,128)}, f32[768,256]{1,0:T(8,128)}) custom-call(bf16[48,4096]{1,0:T(8,128)(2,1)} %bitcast.42, f32[768,256]{1,0:T(8,128)} %bitcast.40, bf16[2,256,4096]{2,1,0:T(8,128)(2,1)} %refs_2_.6, bf16[2,4096]{1,0:T(2,128)(2,1)} %refs_3_.5, bf16[3,4096,768]{2,1,0:T(8,128)(2,1)} %refs_4_.7, ...), custom_call_target="tpu_custom_call" | custom-call | flops 19327352832 | bytes 12884901 | tf_op jit(solution)/shard_map/ring_1/pallas_call | solution.py:346
  202.2 5.1 %recurrence_1.1 = (f32[16,6,8,256]{3,2,1,0:T(8,128)}, bf16[6,3,256]{2,1,0:T(4,128)(2,1)}, f32[6,256]{1,0:T(8,128)}) custom-call(f32[16,6,8,256]{3,2,1,0:T(8,128)} %bitcast.27, f32[16,6,8,256]{3,2,1,0:T(8,128)} %bitcast.28, s32[6,128,1]{2,1,0:T(8,128)} %copy.44.pos_ref.pos_col_ref, bf16[2,6,3,256]{3,2,1,0:T(4,128)(2,1)} %copy.45.cs_ref, ...), custom_call_target="tpu_custom_call" | custom-call | flops 201326592 | bytes 3145728 | tf_op jit(solution)/shard_map/recurrence_1/pallas_call | solution.py:411
  207.4 0.1 convert_element_type.28
  207.5 0.1 convert_element_type.30
  207.6 1.4 fusion
  209.0 1.2 pad_maximum_fusion
  210.2 148.8 %ring_2.1 = (bf16[48,4096]{1,0:T(8,128)(2,1)}, f32[768,256]{1,0:T(8,128)}, f32[768,256]{1,0:T(8,128)}, f32[768,256]{1,0:T(8,128)}) custom-call(bf16[48,4096]{1,0:T(8,128)(2,1)} %get-tuple-element.28.refs_0_, f32[768,256]{1,0:T(8,128)} %bitcast.39, bf16[2,256,4096]{2,1,0:T(8,128)(2,1)} %refs_2_.6, bf16[2,4096]{1,0:T(2,128)(2,1)} %refs_3_.5, ...), custom_call_target="tpu_custom_call" | custom-call | flops 20937965568 | bytes 13958643 | tf_op jit(solution)/shard_map/ring_2/pallas_call | solution.py:346
  359.0 0.7 broadcast_in_dim.21.slot_ref
  359.7 0.6 broadcast_in_dim.22.pos_row_ref
  360.3 0.3 reduce_window_sum.11
  360.6 0.6 broadcast_in_dim.23.doc_row_ref
  361.2 1.0 copy.52.doc_col_ref
  362.1 16.0 %attention.1 = (f32[16,6,8,256]{3,2,1,0:T(8,128)}, bf16[6,2048,256]{2,1,0:T(8,128)(2,1)}, bf16[6,2048,256]{2,1,0:T(8,128)(2,1)}, s32[6,1,2048]{2,1,0:T(1,128)}) custom-call(f32[16,6,8,256]{3,2,1,0:T(8,128)} %bitcast.24, f32[16,6,8,256]{3,2,1,0:T(8,128)} %bitcast.25, f32[16,6,8,256]{3,2,1,0:T(8,128)} %bitcast.26, bf16[6,2048,256]{2,1,0:T(8,128)(2,1)} %kc_ref.1, ...), custom_call_target="tpu_custom_call" | custom-call | flops 3221225472 | bytes 25165824 | tf_op jit(solution)/shard_map/attention/pallas_call | solution.py:471
  378.1 0.6 broadcast_in_dim.25.refs_3_
  378.7 112.0 %ring_3.1 = bf16[48,4096]{1,0:T(8,128)(2,1)} custom-call(bf16[48,4096]{1,0:T(8,128)(2,1)} %get-tuple-element.32.refs_0_, f32[768,256]{1,0:T(8,128)} %bitcast.23, bf16[256,4096]{1,0:T(8,128)(2,1)} %refs_2_.7, bf16[1,4096]{1,0:T(2,128)(2,1)} %broadcast_in_dim.25.refs_3_, bf16[3,4096,768]{2,1,0:T(8,128)(2,1)} %refs_4_.7, bf16[3,4096,768]{2,1,0:T(8,128)(2,1)} %refs_5_.7, ...), custom_call_target="tpu_custom_call" | custom-call | flops 16106127360 | bytes 10737418 | tf_op jit(solution)/shard_map/ring_3/pallas_call | solution.py:346
  490.7 0.6 copy.53
  491.4 0.0 copy-done.8
  491.4 0.6 copy.54
  492.0 0.6 copy.57
  492.6 1.8 copy.59
  (21 shorter events, 0.1 us)
Async XLA Ops:
  0.6 46.0 %copy-start = (s32[6,128]{1,0:T(8,128)S(1)}, s32[6,128]{1,0:T(8,128)}, u32[]{:S(2)}) copy-start(s32[6,128]{1,0:T(8,128)} %param.33) | copy-start | bytes 9220
  0.6 46.9 %copy-start.3 = (bf16[2,6,3,256]{3,0,2,1:T(2,128)(2,1)S(1)}, bf16[2,6,3,256]{3,0,2,1:T(2,128)(2,1)}, u32[]{:S(2)}) copy-start(bf16[2,6,3,256]{3,0,2,1:T(2,128)(2,1)} %param.34) | copy-start | bytes 55300
  0.7 47.5 %copy-start.4 = (f32[2,6,256]{2,0,1:T(2,128)S(1)}, f32[2,6,256]{2,0,1:T(2,128)}, u32[]{:S(2)}) copy-start(f32[2,6,256]{2,0,1:T(2,128)} %param.35) | copy-start | bytes 36868
  0.7 48.1 %copy-start.10 = (f32[2,256]{1,0:T(2,128)S(1)}, f32[2,256]{1,0:T(2,128)}, u32[]{:S(2)}) copy-start(f32[2,256]{1,0:T(2,128)} %param.50) | copy-start | bytes 6148
  210.2 148.8 %copy-start.1 = (s32[6,2048]{1,0:T(8,128)S(1)}, s32[6,2048]{1,0:T(8,128)}, u32[]{:S(2)}) copy-start(s32[6,2048]{1,0:T(8,128)} %param.38) | copy-start | bytes 147460
  362.1 16.0 %copy-start.7 = (bf16[4096]{0:T(1024)(128)(2,1)S(1)}, bf16[4096]{0:T(1024)(128)(2,1)}, u32[]{:S(2)}) copy-start(bf16[4096]{0:T(1024)(128)(2,1)} %param.57) | copy-start | bytes 24580
  378.7 112.0 %copy-start.5 = (bf16[6,3,256]{2,1,0:T(4,128)(2,1)S(1)}, bf16[6,3,256]{2,1,0:T(4,128)(2,1)}, u32[]{:S(2)}) copy-start(bf16[6,3,256]{2,1,0:T(4,128)(2,1)} %get-tuple-element.37) | copy-start | bytes 27652
  378.7 112.0 %copy-start.6 = (bf16[6,3,256]{2,1,0:T(4,128)(2,1)S(1)}, bf16[6,3,256]{2,1,0:T(4,128)(2,1)}, u32[]{:S(2)}) copy-start(bf16[6,3,256]{2,1,0:T(4,128)(2,1)} %get-tuple-element.38) | copy-start | bytes 27652
  378.7 112.7 %copy-start.8 = (f32[6,256]{1,0:T(8,128)S(1)}, f32[6,256]{1,0:T(8,128)}, u32[]{:S(2)}) copy-start(f32[6,256]{1,0:T(8,128)} %get-tuple-element.39) | copy-start | bytes 18436
  378.7 112.7 %copy-start.9 = (f32[6,256]{1,0:T(8,128)S(1)}, f32[6,256]{1,0:T(8,128)}, u32[]{:S(2)}) copy-start(f32[6,256]{1,0:T(8,128)} %get-tuple-element.40) | copy-start | bytes 18436
  378.7 113.3 %copy-start.2 = (s32[6,1,2048]{2,1,0:T(1,128)S(1)}, s32[6,1,2048]{2,1,0:T(1,128)}, u32[]{:S(2)}) copy-start(s32[6,1,2048]{2,1,0:T(1,128)} %get-tuple-element.43) | copy-start | bytes 147460

commit v2 on v1

--- a/solution.py
+++ b/solution.py
@@ -17,10 +17,7 @@
 BF16 = jnp.bfloat16
 
 SLOT_REL = (0, -1, 1, -2, 2, -3, 3, 4)
-NC = 4
-HALF = NC // 2
-UP_ORDER = (0, 1, 2, 3)
-DOWN_ORDER = (2, 3, 0, 1)
+ROW_TILE = 16
 
 
 def slot_of(rel):
@@ -32,7 +29,7 @@
 
 
 class Net:
-    def __init__(self, tp, rows, dim, g, pown, dsend, drecv, zsend, zrecv, ag_z, ag_d, rs_z, rs_d, send_z, send_d):
+    def __init__(self, tp, rows, dim, r):
         self.me = lax.axis_index('tp')
         self.core = lax.rem(self.me, 2)
         self.chips = tp // 2
@@ -41,10 +38,10 @@
         self.down = lax.rem(self.me + tp - 2, tp)
         self.partner = self.me + 1 - 2 * self.core
         self.rows = rows
+        self.groups = rows // ROW_TILE
         self.dim = dim
-        self.cw = dim // NC
-        self.g, self.pown, self.dsend, self.drecv, self.zsend, self.zrecv = g, pown, dsend, drecv, zsend, zrecv
-        self.ag_z, self.ag_d, self.rs_z, self.rs_d, self.send_z, self.send_d = ag_z, ag_d, rs_z, rs_d, send_z, send_d
+        self.cw = dim // 2
+        self.r = r
 
     def barrier(self):
         sem = pltpu.get_barrier_semaphore()
@@ -52,139 +49,163 @@
             pl.semaphore_signal(sem, inc=1, device_id={'tp': other}, device_id_type=pl.DeviceIdType.MESH)
         pl.semaphore_wait(sem, 3)
 
-    def cols(self, ch):
-        return pl.ds(ch * self.cw, self.cw)
+    def span(self, chunk):
+        half, group = chunk
+        cols = half * self.cw
+        if not isinstance(half, int):
+            cols = pl.multiple_of(cols, 128)
+        return pl.ds(group * ROW_TILE, ROW_TILE), pl.ds(cols, self.cw)
 
     def remote(self, src, dst, send, recv, dev):
         return pltpu.make_async_remote_copy(src_ref=src, dst_ref=dst, send_sem=send, recv_sem=recv, device_id={'tp': dev}, device_id_type=pl.DeviceIdType.MESH)
 
-    def ag_hop(self, way, d, ch):
+    def ag_hop(self, way, d, chunk):
         sign = -1 if way == 0 else 1
         src, dst = slot_of(sign * (d - 1)), slot_of(sign * d)
-        return self.remote(self.g.at[2 * src + self.core, :, self.cols(ch)], self.g.at[2 * dst + self.core, :, self.cols(ch)],
-                           self.send_z.at[way, d - 1, ch], self.ag_z.at[way, d - 1, ch], self.up if way == 0 else self.down)
-
-    def ag_pair(self, slot, ch):
-        ref = self.g.at[2 * slot + self.core, :, self.cols(ch)]
-        return self.remote(ref, ref, self.send_d.at[slot, ch], self.ag_d.at[slot, ch], self.partner)
-
-    def rs_pair(self, slot, ch):
-        return self.remote(self.dsend.at[slot, :, self.cols(ch)], self.drecv.at[slot, :, self.cols(ch)],
-                           self.send_d.at[slot, ch], self.rs_d.at[slot, ch], self.partner)
-
-    def rs_hop(self, way, d, ch):
-        return self.remote(self.zsend.at[way, d - 1, :, self.cols(ch)], self.zrecv.at[way, d - 1, :, self.cols(ch)],
-                           self.send_z.at[way, d - 1, ch], self.rs_z.at[way, d - 1, ch], self.up if way == 0 else self.down)
-
-    def last_hop(self, way, ch):
-        return ch < HALF if way == 0 else ch >= HALF
+        g, sems = self.r['g'], (way, d - 1) + chunk
+        return self.remote(g.at[(2 * src + self.core,) + self.span(chunk)], g.at[(2 * dst + self.core,) + self.span(chunk)],
+                           self.r['send_z'].at[sems], self.r['ag_z'].at[sems], self.up if way == 0 else self.down)
+
+    def ag_pair(self, slot, chunk):
+        ref, sems = self.r['g'].at[(2 * slot + self.core,) + self.span(chunk)], (slot,) + chunk
+        return self.remote(ref, ref, self.r['send_d'].at[sems], self.r['ag_d'].at[sems], self.partner)
+
+    def rs_pair(self, slot, chunk):
+        idx, sems = (slot,) + self.span(chunk), (slot,) + chunk
+        return self.remote(self.r['dsend'].at[idx], self.r['drecv'].at[idx], self.r['give_d'].at[sems], self.r['rs_d'].at[sems], self.partner)
+
+    def rs_hop(self, way, d, chunk):
+        idx, sems = (way, d - 1) + self.span(chunk), (way, d - 1) + chunk
+        return self.remote(self.r['zsend'].at[idx], self.r['zrecv'].at[idx], self.r['give_z'].at[sems], self.r['rs_z'].at[sems], self.up if way == 0 else self.down)
+
+    def chunks(self):
+        return [(half, group) for group in range(self.groups) for half in range(2)]
 
     def hops(self):
         for way in range(2):
             for d in range(1, 5):
-                for ch in range(NC):
-                    if d < 4 or self.last_hop(way, ch):
-                        yield way, d, ch
+                for chunk in self.chunks():
+                    if d < 4 or chunk[0] == way:
+                        yield way, d, chunk
 
     def abs_chip(self, rel):
         return lax.rem(self.chip + (rel + self.chips), self.chips)
 
     def wait_pair(self, slots):
         for slot in slots:
-            for ch in range(NC):
-                self.ag_pair(slot, ch).wait_recv()
+            for chunk in self.chunks():
+                self.ag_pair(slot, chunk).wait_recv()
+
+    def gather_start(self, group):
+        for k in range(2):
+            self.ag_hop(0, 1, (k, group)).start()
+            self.ag_hop(1, 1, (1 - k, group)).start()
+        for k in range(2):
+            self.ag_pair(0, (k, group)).start()
 
     def gather(self, run_pass):
-        for p in range(NC):
-            self.ag_hop(0, 1, UP_ORDER[p]).start()
-            self.ag_hop(1, 1, DOWN_ORDER[p]).start()
-        for ch in range(NC):
-            self.ag_pair(0, ch).start()
         self.wait_pair((0,))
         run_pass(0, 1)
         for d in range(1, 5):
-            for p in range(NC if d < 4 else HALF):
-                for way, order in ((0, UP_ORDER), (1, DOWN_ORDER)):
-                    ch = order[p]
-                    self.ag_hop(way, d, ch).wait_recv()
-                    if d < 3 or (d == 3 and self.last_hop(way, ch)):
-                        self.ag_hop(way, d + 1, ch).start()
-                    self.ag_pair(slot_of(-d if way == 0 else d), ch).start()
+            for p in range(2 * self.groups if d < 4 else self.groups):
+                for way in range(2):
+                    chunk = ((p + way) % 2, p // 2) if d < 4 else (way, p)
+                    self.ag_hop(way, d, chunk).wait_recv()
+                    if d < 3 or (d == 3 and chunk[0] == way):
+                        self.ag_hop(way, d + 1, chunk).start()
+                    self.ag_pair(slot_of(-d if way == 0 else d), chunk).start()
                 if p == 0 and d > 1:
                     self.wait_pair((2 * d - 3, 2 * d - 2))
                     run_pass(2 * d - 3, 2 * d - 1)
+
+    def gather_end(self, run_pass):
         self.wait_pair((7,))
         run_pass(7, 8)
-        for way, d, ch in self.hops():
-            self.ag_hop(way, d, ch).wait_send()
+        for way, d, chunk in self.hops():
+            self.ag_hop(way, d, chunk).wait_send()
         for slot in range(8):
-            for ch in range(NC):
-                self.ag_pair(slot, ch).wait_send()
-
-    def reduce(self, lhs_of, w_ref, finish):
-        rows = self.rows
+            for chunk in self.chunks():
+                self.ag_pair(slot, chunk).wait_send()
+
+    def reduce(self, lhs_of, w_ref, finish, between=None):
+        r, rows = self.r, self.rows
         sub = min(512, self.cw)
+        steps = self.cw // sub
 
         def slots_of(d):
             return {4: (7,), 0: (0,)}.get(d, (slot_of(-d), slot_of(d)))
 
-        def compute(d, ch):
+        def compute(d):
             slots = slots_of(d)
-            lhs = jnp.concatenate([lhs_of(s, self.core) for s in slots] + [lhs_of(s, 1 - self.core) for s in slots], axis=0)
-            for t in range(self.cw // sub):
-                span = pl.ds(ch * self.cw + t * sub, sub)
-                out = jnp.dot(lhs, w_ref[:, span], preferred_element_type=F32)
-                for i, s in enumerate(slots):
-                    self.pown[s, :, span] = out[i * rows:(i + 1) * rows]
-                    self.dsend[s, :, span] = out[(len(slots) + i) * rows:(len(slots) + i + 1) * rows].astype(BF16)
-            for s in slots:
-                self.rs_pair(s, ch).start()
-
-        def combine(way, d, ch):
+            for half in range(2):
+                def body(t, carry):
+                    span = pl.ds(pl.multiple_of(half * self.cw + t * sub, sub), sub)
+                    lhs = jnp.concatenate([lhs_of(s, self.core) for s in slots] + [lhs_of(s, 1 - self.core) for s in slots], axis=0)
+                    out = jnp.dot(lhs, w_ref[:, span], preferred_element_type=F32)
+                    for i, s in enumerate(slots):
+                        j = len(slots) + i
+                        r['pown'][s, :, span] = out[i * rows:(i + 1) * rows]
+                        r['dsend'][s, :, span] = out[j * rows:(j + 1) * rows].astype(BF16)
+                    return carry
+                lax.fori_loop(0, steps, body, 0)
+                for group in range(self.groups):
+                    for s in slots:
+                        self.rs_pair(s, (half, group)).start()
+
+        def combine(way, d, chunk):
             s = slot_of(d if way == 0 else -d)
-            self.rs_pair(s, ch).wait_recv()
-            total = self.pown[s, :, self.cols(ch)] + self.drecv[s, :, self.cols(ch)].astype(F32)
-            if d < 3 or (d == 3 and self.last_hop(way, ch)):
-                self.rs_hop(way, d + 1, ch).wait_recv()
-                total = total + self.zrecv[way, d, :, self.cols(ch)].astype(F32)
-            self.zsend[way, d - 1, :, self.cols(ch)] = total.astype(BF16)
-            self.rs_hop(way, d, ch).start()
-
-        order = tuple(x for i in range(HALF) for x in (i, i + HALF))
-        for ch in order:
-            compute(4, ch)
-        for ch in order[:HALF]:
-            compute(3, ch)
-        for p in range(HALF):
-            combine(0, 4, p)
-            combine(1, 4, HALF + p)
-        for ch in order[HALF:]:
-            compute(3, ch)
-        for d in (3, 2, 1):
-            for p in range(NC):
-                combine(0, d, (p + HALF) % NC)
-                combine(1, d, p)
-                compute(d - 1, order[p])
-        for ch in range(NC):
-            self.rs_pair(0, ch).wait_recv()
-            self.rs_hop(0, 1, ch).wait_recv()
-            self.rs_hop(1, 1, ch).wait_recv()
-            total = self.pown[0, :, self.cols(ch)] + self.drecv[0, :, self.cols(ch)].astype(F32)
-            total = total + self.zrecv[0, 0, :, self.cols(ch)].astype(F32) + self.zrecv[1, 0, :, self.cols(ch)].astype(F32)
-            finish(self.cols(ch), total)
-        for way, d, ch in self.hops():
-            self.rs_hop(way, d, ch).wait_send()
+            idx = self.span(chunk)
+            self.rs_pair(s, chunk).wait_recv()
+            total = r['pown'][(s,) + idx] + r['drecv'][(s,) + idx].astype(F32)
+            if d < 3 or (d == 3 and chunk[0] == way):
+                self.rs_hop(way, d + 1, chunk).wait_recv()
+                total = total + r['zrecv'][(way, d) + idx].astype(F32)
+            r['zsend'][(way, d - 1) + idx] = total.astype(BF16)
+            self.rs_hop(way, d, chunk).start()
+
+        def send(d, deep):
+            for group in range(self.groups):
+                for way in range(2):
+                    combine(way, d, (way if deep else 1 - way, group))
+
+        compute(3)
+        send(3, False)
+        compute(2)
+        if between is not None:
+            between()
+        compute(4)
+        send(2, False)
+        send(4, True)
+        compute(1)
+        send(3, True)
+        send(1, False)
+        compute(0)
+        send(2, True)
+        send(1, True)
+        for group in range(self.groups):
+            for half in range(2):
+                self.rs_pair(0, (half, group)).wait_recv()
+                self.rs_hop(0, 1, (half, group)).wait_recv()
+                self.rs_hop(1, 1, (half, group)).wait_recv()
+                idx = self.span((half, group))
+                total = r['pown'][(0,) + idx] + r['drecv'][(0,) + idx].astype(F32)
+                total = total + r['zrecv'][(0, 0) + idx].astype(F32) + r['zrecv'][(1, 0) + idx].astype(F32)
+                finish(idx, total)
+            yield group
+
+    def reduce_end(self):
+        for way, d, chunk in self.hops():
+            self.rs_hop(way, d, chunk).wait_send()
         for slot in range(8):
-            for ch in range(NC):
-                self.rs_pair(slot, ch).wait_send()
+            for chunk in self.chunks():
+                self.rs_pair(slot, chunk).wait_send()
 
 
 def comm_kernel(cfg, names, outs, scratch, *refs):
     r = dict(zip(names + outs + scratch, refs))
     x_ref = r['x']
     rows, dim = x_ref.shape
-    net = Net(cfg['tp'], rows, dim, r['g'], r.get('pown'), r.get('dsend'), r.get('drecv'), r.get('zsend'), r.get('zrecv'),
-              r['ag_z'], r['ag_d'], r['rs_z'], r['rs_d'], r['send_z'], r['send_d'])
+    net = Net(cfg['tp'], rows, dim, r)
     loads = {}
     for i, (key, src, layer) in enumerate(cfg['loads']):
         view = r[src] if layer is None else r[src].at[layer]
@@ -193,28 +214,30 @@
     net.barrier()
     xbuf = r['xbuf']
     xbuf[...] = x_ref[...]
-    eps = 1e-6
-
-    def normalize(idx):
-        gain = 1.0 + r['norm'][idx:idx + 1, :].astype(F32)
-
-        def body(i, carry):
-            span = pl.ds(pl.multiple_of(i * 16, 16), 16)
-            h = xbuf[span, :].astype(F32)
-            inv = lax.rsqrt(jnp.mean(h * h, axis=-1, keepdims=True) + eps)
-            r['g'][net.core, span, :] = (h * inv * gain).astype(BF16)
-            return carry
-        lax.fori_loop(0, rows // 16, body, 0)
+    groups = range(net.groups)
+
+    def normalize(idx, group):
+        span = pl.ds(group * ROW_TILE, ROW_TILE)
+        h = xbuf[span, :].astype(F32)
+        inv = lax.rsqrt(jnp.mean(h * h, axis=-1, keepdims=True) + 1e-6)
+        r['g'][net.core, span, :] = (h * inv * (1.0 + r['norm'][idx:idx + 1, :].astype(F32))).astype(BF16)
 
     def finish_with(bias_ref, idx):
-        def finish(cols, total):
-            bias = bias_ref[idx:idx + 1, cols].astype(F32)
-            xbuf[:, cols] = (xbuf[:, cols].astype(F32) + total + bias).astype(BF16)
+        def finish(span, total):
+            xbuf[span] = (xbuf[span].astype(F32) + total + bias_ref[idx:idx + 1, span[1]].astype(F32)).astype(BF16)
         return finish
 
     def block_of(first, last):
         return r['g'][2 * first:2 * last].reshape((last - first) * 2 * rows, dim)
 
+    def enter(idx, steps=None):
+        for group in groups if steps is None else steps:
+            normalize(idx, group)
+            net.gather_start(group)
+        if steps is not None:
+            net.reduce_end()
+
+    reduction = None
     if cfg['pre'] is not None:
         r['apre'][...] = r['mid'][...].astype(BF16)
         loads['w_pre'].wait()
@@ -222,18 +245,16 @@
         def lhs_pre(slot, core):
             blk = 2 * net.abs_chip(SLOT_REL[slot]) + core
             return r['apre'][pl.ds(pl.multiple_of(blk * rows, 16), rows), :]
-        net.reduce(lhs_pre, r['w_pre'], finish_with(r['b_pre'], cfg['pre']))
+        reduction = net.reduce(lhs_pre, r['w_pre'], finish_with(r['b_pre'], cfg['pre']))
 
     if cfg['mlp'] is not None:
         m = cfg['mlp']
-        normalize(2 * m + 1)
-        pending = ['w_1s', 'w_2s']
+        pending = ['w_1s', 'w_2s', 'w_ds']
 
         def mlp_pass(first, last):
             while pending:
                 loads[pending.pop()].wait()
             count = 2 * (last - first)
-            ff = r['w_1s'].shape[1]
 
             def body(t, carry):
                 cols = pl.ds(pl.multiple_of(t * 256, 256), 256)
@@ -243,14 +264,13 @@
                 act = (jax.nn.gelu(h1, approximate=True) * h2).astype(BF16)
                 r['act'][2 * first:2 * last, :, cols] = act.reshape(count, rows, 256)
                 return carry
-            lax.fori_loop(0, ff // 256, body, 0)
+            lax.fori_loop(0, r['w_1s'].shape[1] // 256, body, 0)
+        enter(2 * m + 1, reduction)
         net.gather(mlp_pass)
-        loads['w_ds'].wait()
-        net.reduce(lambda slot, core: r['act'][2 * slot + core], r['w_ds'], finish_with(r['b_d'], m))
+        reduction = net.reduce(lambda slot, core: r['act'][2 * slot + core], r['w_ds'], finish_with(r['b_d'], m), lambda: net.gather_end(mlp_pass))
 
     if cfg['post'] is not None:
         kind, idx = cfg['post']
-        normalize(4 if kind == 'attn' else 2 * idx)
         waiting = [key for key, _, _ in cfg['loads'] if key.startswith('p_')]
 
         def post_pass(first, last):
@@ -274,7 +294,13 @@
                 put(r['o_q'], jnp.dot(lhs, r['p_q'][...], preferred_element_type=F32), True)
                 put(r['o_k'], jnp.dot(lhs, r['p_k'][...], preferred_element_type=F32), True)
                 put(r['o_v'], jnp.dot(lhs, r['p_v'][...], preferred_element_type=F32))
+        enter(4 if kind == 'attn' else 2 * idx, reduction)
         net.gather(post_pass)
+        net.gather_end(post_pass)
+    else:
+        for _ in reduction:
+            pass
+        net.reduce_end()
     if 'o_x' in r:
         r['o_x'][...] = xbuf[...]
 
@@ -336,10 +362,10 @@
             add(key, value, vmem)
     scratch['g'] = pltpu.VMEM((tp, rows, dim), BF16)
     scratch['xbuf'] = pltpu.VMEM((rows, dim), BF16)
-    for key in ('ag_z', 'rs_z', 'send_z'):
-        scratch[key] = pltpu.SemaphoreType.DMA((2, 4, NC))
-    for key in ('ag_d', 'rs_d', 'send_d'):
-        scratch[key] = pltpu.SemaphoreType.DMA((8, NC))
+    for key in ('ag_z', 'rs_z', 'send_z', 'give_z'):
+        scratch[key] = pltpu.SemaphoreType.DMA((2, 4, 2, rows // ROW_TILE))
+    for key in ('ag_d', 'rs_d', 'send_d', 'give_d'):
+        scratch[key] = pltpu.SemaphoreType.DMA((8, 2, rows // ROW_TILE))
     scratch['w_sem'] = pltpu.SemaphoreType.DMA((len(loads),))
     cfg = dict(tp=tp, loads=tuple(loads), pre=None if pre is None else pre[1], mlp=None if mlp is None else mlp[0],
                post=None if post is None else (post[0], post[1]))
@@ -356,6 +382,11 @@
     return dict(zip(outs, result))
 
 
+def column_of(row):
+    n = row.shape[1]
+    return jnp.broadcast_to(row, (n, n)).T[:, :1]
+
+
 def rec_kernel(layer, seqs, u_ref, y_ref, pos_ref, cs_ref, ls_ref, cw_ref, cb_ref, wa_ref, ba_ref, wi_ref, bi_ref, sp_ref, hy_ref, co_ref, lo_ref, pad):
     blocks = u_ref.shape[0]
     toks = blocks * 8
@@ -373,7 +404,7 @@
         gate_r = jax.nn.sigmoid(jnp.dot(conv, wa_ref[0], preferred_element_type=F32) + ba_ref[layer:layer + 1, :].astype(F32))
         gate_i = jax.nn.sigmoid(jnp.dot(conv, wi_ref[0], preferred_element_type=F32) + bi_ref[layer:layer + 1, :].astype(F32))
         decay = jnp.exp(-8.0 * gate_r * sp_ref[layer:layer + 1, :])
-        reset = pos_ref[s] == 0
+        reset = column_of(pos_ref[pl.ds(s, 1), :]) == 0
         mult = jnp.where(reset, 1.0, jnp.sqrt(1.0 - decay * decay))
         decay = jnp.where(reset, 0.0, decay)
         drive = conv.astype(F32) * gate_i * mult
@@ -396,9 +427,8 @@
     lax.fori_loop(0, seqs, one_seq, 0)
 
 
-def rec_call(layer, u, y, pos_col, conv_state, lru_state, conv_w, conv_b, w_a, b_a, w_i, b_i, soft):
-    seqs = pos_col.shape[0]
-    toks = pos_col.shape[1]
+def rec_call(layer, u, y, seg_pos, conv_state, lru_state, conv_w, conv_b, w_a, b_a, w_i, b_i, soft):
+    seqs, toks = seg_pos.shape
     width = u.shape[-1]
     blocks = toks // 8
     shape4 = (blocks, seqs, 8, width)
@@ -406,7 +436,7 @@
     layer_spec = lambda a: pl.BlockSpec((None,) + a.shape[1:], functools.partial(lambda n, i: (layer,) + (0,) * n, a.ndim - 1))
     whole = lambda a: pl.BlockSpec(a.shape, functools.partial(lambda n, i: (0,) * n, a.ndim))
     out_shape = (jax.ShapeDtypeStruct(shape4, F32), jax.ShapeDtypeStruct((seqs, 3, width), BF16), jax.ShapeDtypeStruct((seqs, width), F32))
-    args = (u.reshape(shape4), y.reshape(shape4), pos_col, conv_state, lru_state, conv_w, conv_b, w_a, b_a, w_i, b_i, soft)
+    args = (u.reshape(shape4), y.reshape(shape4), seg_pos, conv_state, lru_state, conv_w, conv_b, w_a, b_a, w_i, b_i, soft)
     per_layer = {3, 4, 7, 9}
     return pl.pallas_call(
         functools.partial(rec_kernel, layer, seqs),
@@ -420,15 +450,22 @@
     )(*args)
 
 
-def attn_kernel(q_ref, k_ref, v_ref, kc_ref, vc_ref, slot_ref, pos_row_ref, pos_col_ref, doc_row_ref, doc_col_ref, o_ref, ko_ref, vo_ref, so_ref):
+def attn_kernel(q_ref, k_ref, v_ref, kc_ref, vc_ref, slot_ref, pos_ref, o_ref, ko_ref, vo_ref, so_ref):
     blocks, _, _, width = q_ref.shape
     toks = blocks * 8
     q = q_ref[...].reshape(toks, width).astype(BF16)
     kn = k_ref[...].reshape(toks, width).astype(BF16)
     vn = v_ref[...].reshape(toks, width).astype(BF16)
     kc, vc = kc_ref[0], vc_ref[0]
-    slot = slot_ref[0]
-    pos_row, pos_col, doc_row, doc_col = pos_row_ref[0], pos_col_ref[0], doc_row_ref[0], doc_col_ref[0]
+    seq = pl.ds(pl.program_id(0), 1)
+    slot, pos_row = slot_ref[seq, :], pos_ref[seq, :]
+    pos_mat = jnp.broadcast_to(pos_row, (toks, toks))
+    pos_mat_t = pos_mat.T
+    pos_col = pos_mat_t[:, :1]
+    row_i = lax.broadcasted_iota(jnp.int32, (toks, toks), 0)
+    col_i = lax.broadcasted_iota(jnp.int32, (toks, toks), 1)
+    doc_col = jnp.sum(jnp.where((pos_mat == 0) & (col_i <= row_i), 1.0, 0.0), axis=1, keepdims=True)
+    doc_row = jnp.sum(jnp.where((pos_mat_t == 0) & (row_i <= col_i), 1.0, 0.0), axis=0, keepdims=True)
     contract = (((1,), (1,)), ((), ()))
     diff_old = pos_col - slot
     keep_old = (slot >= 0) & (diff_old >= 0) & (diff_old < WINDOW) & (doc_col == 0)
@@ -454,7 +491,7 @@
     vo_ref[0] = jnp.where(any_hit, jnp.dot(pick, vn, preferred_element_type=F32), vc.astype(F32)).astype(BF16)
     hit_t = lax.broadcasted_iota(jnp.int32, (toks, window), 1) == target_col
     newest = jnp.max(jnp.where(hit_t, pos_col, -1), axis=0, keepdims=True)
-    so_ref[0] = jnp.where(newest >= 0, newest, slot)
+    so_ref[seq, :] = jnp.where(newest >= 0, newest, slot)
 
 
 def attn_call(q, k, v, k_cache, v_cache, slot_pos, seg_pos):
@@ -463,21 +500,19 @@
     blocks = toks // 8
     window = k_cache.shape[1]
     shape4 = (blocks, seqs, 8, width)
-    doc = jnp.cumsum((seg_pos == 0).astype(jnp.int32), axis=1)
     tok_spec = pl.BlockSpec((blocks, 1, 8, width), lambda s: (0, s, 0, 0))
     cache_spec = pl.BlockSpec((1, window, width), lambda s: (s, 0, 0))
-    row_spec = lambda n: pl.BlockSpec((1, 1, n), lambda s: (s, 0, 0))
-    col_spec = pl.BlockSpec((1, toks, 1), lambda s: (s, 0, 0))
+    row_spec = lambda n: pl.BlockSpec((seqs, n), lambda s: (0, 0))
     out, k_out, v_out, slot_out = pl.pallas_call(
         attn_kernel,
         grid=(seqs,),
-        out_shape=(jax.ShapeDtypeStruct(shape4, F32), jax.ShapeDtypeStruct(k_cache.shape, BF16), jax.ShapeDtypeStruct(v_cache.shape, BF16), jax.ShapeDtypeStruct((seqs, 1, window), jnp.int32)),
-        in_specs=[tok_spec, tok_spec, tok_spec, cache_spec, cache_spec, row_spec(window), row_spec(toks), col_spec, row_spec(toks), col_spec],
+        out_shape=(jax.ShapeDtypeStruct(shape4, F32), jax.ShapeDtypeStruct(k_cache.shape, BF16), jax.ShapeDtypeStruct(v_cache.shape, BF16), jax.ShapeDtypeStruct((seqs, window), jnp.int32)),
+        in_specs=[tok_spec, tok_spec, tok_spec, cache_spec, cache_spec, row_spec(window), row_spec(toks)],
         out_specs=(tok_spec, cache_spec, cache_spec, row_spec(window)),
         cost_estimate=pl.CostEstimate(flops=8 * seqs * toks * window * width, bytes_accessed=8 * seqs * window * width, transcendentals=0),
         name='attention',
-    )(q.reshape(shape4), k.reshape(shape4), v.reshape(shape4), k_cache, v_cache, slot_pos[:, None, :], seg_pos[:, None, :], seg_pos[:, :, None], doc[:, None, :], doc[:, :, None])
-    return out.reshape(blocks * seqs * 8, width), k_out, v_out, slot_out.reshape(slot_pos.shape)
+    )(q.reshape(shape4), k.reshape(shape4), v.reshape(shape4), k_cache, v_cache, slot_pos, seg_pos)
+    return out.reshape(blocks * seqs * 8, width), k_out, v_out, slot_out
 
 
 def solution(mesh):
@@ -487,7 +522,6 @@
         seqs, toks = seg_pos.shape
         dim = x_in.shape[-1]
         x = x_in.reshape(-1, dim)
-        pos_col = seg_pos[:, :, None]
         soft = jax.nn.softplus(a_param)
         half = ROPE_DIM // 2
         timescale = 10000.0 ** (2.0 * jnp.arange(half).astype(F32) / ROPE_DIM)
@@ -506,7 +540,7 @@
         conv_list, lru_list = [], []
         out = comm_call(tp, 0, x, post=rec_post(0))
         for layer in range(2):
-            mid, conv_new, lru_new = rec_call(layer, out['o_u'], out['o_y'], pos_col, conv_state, lru_state, conv_w, conv_b, w_a, b_a, w_i, b_i, soft)
+            mid, conv_new, lru_new = rec_call(layer, out['o_u'], out['o_y'], seg_pos, conv_state, lru_state, conv_w, conv_b, w_a, b_a, w_i, b_i, soft)
             conv_list.append(conv_new)
             lru_list.append(lru_new)
             post = rec_post(1) if layer == 0 else ('attn', 0, norm_scale, (('p_q', w_q, None), ('p_k', w_k, None), ('p_v', w_v, None)), (('cos', cos2), ('sin', sin2)))

time: 504 us -> 493 us (0.978)
  no operation moved by 1% of the time
where the time goes in v2:
time: 493 us; the launch traced here: 488 us
  Pallas kernels  479 us (97%)
  local copies, waits for them, and re-layouts  5.06 us (1%)
    pallas_call x4, Pallas kernels, comm_call(): pl.pallas_call(functools.partial(comm_kernel, cfg, names, list(outs), lis...  453 us
    pallas_call x1, Pallas kernels, attn_call(): pl.pallas_call(attn_kernel, grid=(seqs,), out_shape=(jax.ShapeDtypeStruct...  15.5 us
    pallas_call x2, Pallas kernels, rec_call(): pl.pallas_call(functools.partial(rec_kernel, layer, seqs), grid=(1,), out...  10.3 us

profile of v2, /device:TPU:21, one launch (start us, length us, event | category | flops | bytes accessed | tf_op | source)
XLA Modules:
  0.0 487.7 jit_solution(1122307786712602932)
XLA Ops:
  0.6 0.0 copy-start.1
  0.6 0.0 copy-start.2
  0.7 0.0 copy-start.8
  0.7 47.2 %ring_0.1 = (f32[768,256]{1,0:T(8,128)}, f32[768,256]{1,0:T(8,128)}) custom-call(bf16[48,4096]{1,0:T(8,128)(2,1)} %bitcast.33, bf16[6,4096]{1,0:T(8,128)(2,1)} %refs_10_.5, bf16[2,4096,256]{2,1,0:T(8,128)(2,1)} %refs_11_.2, bf16[2,4096,256]{2,1,0:T(8,128)(2,1)} %refs_12_.2, bf16[2,256]{1,0:T(2,128)(2,1)} %refs_13_.2, bf16[2,256]{1,0:T(2,128)(2,1)} %refs_14_.1), custom_call_target="tpu_custom_call" | custom-call | flops 3221225472 | bytes 2147483 | tf_op jit(solution)/shard_map/ring_0/pallas_call | solution.py:372
  47.9 0.0 copy-done.1
  47.9 0.6 copy.44.cs_ref
  48.5 0.0 copy-done.2
  48.5 0.6 copy.45.ls_ref
  49.1 0.0 copy-done.8
  49.2 0.6 compare_select_fusion.sp_ref
  49.7 5.2 %recurrence_0.1 = (f32[16,6,8,256]{3,2,1,0:T(8,128)}, bf16[6,3,256]{2,1,0:T(4,128)(2,1)}, f32[6,256]{1,0:T(8,128)}) custom-call(f32[16,6,8,256]{3,2,1,0:T(8,128)} %bitcast.24, f32[16,6,8,256]{3,2,1,0:T(8,128)} %bitcast.25, s32[6,128]{1,0:T(8,128)} %pos_ref.5, bf16[2,6,3,256]{3,2,1,0:T(4,128)(2,1)} %copy.44.cs_ref, f32[2,6,256]{2,1,0:T(8,128)} %copy.45.ls_ref, ...), custom_call_target="tpu_custom_call" | custom-call | flops 201326592 | bytes 3145728 | tf_op jit(solution)/shard_map/recurrence_0/pallas_call | solution.py:441
  55.0 0.0 copy-start
  55.0 145.4 %ring_1.1 = (bf16[48,4096]{1,0:T(8,128)(2,1)}, f32[768,256]{1,0:T(8,128)}, f32[768,256]{1,0:T(8,128)}) custom-call(bf16[48,4096]{1,0:T(8,128)(2,1)} %bitcast.34, f32[768,256]{1,0:T(8,128)} %bitcast.32, bf16[2,256,4096]{2,1,0:T(8,128)(2,1)} %refs_2_.6, bf16[2,4096]{1,0:T(2,128)(2,1)} %refs_3_.5, bf16[3,4096,768]{2,1,0:T(8,128)(2,1)} %refs_4_.7, ...), custom_call_target="tpu_custom_call" | custom-call | flops 19327352832 | bytes 12884901 | tf_op jit(solution)/shard_map/ring_1/pallas_call | solution.py:372
  200.4 5.0 %recurrence_1.1 = (f32[16,6,8,256]{3,2,1,0:T(8,128)}, bf16[6,3,256]{2,1,0:T(4,128)(2,1)}, f32[6,256]{1,0:T(8,128)}) custom-call(f32[16,6,8,256]{3,2,1,0:T(8,128)} %bitcast.22, f32[16,6,8,256]{3,2,1,0:T(8,128)} %bitcast.23, s32[6,128]{1,0:T(8,128)} %pos_ref.5, bf16[2,6,3,256]{3,2,1,0:T(4,128)(2,1)} %copy.44.cs_ref, f32[2,6,256]{2,1,0:T(8,128)} %copy.45.ls_ref, ...), custom_call_target="tpu_custom_call" | custom-call | flops 201326592 | bytes 3145728 | tf_op jit(solution)/shard_map/recurrence_1/pallas_call | solution.py:441
  205.4 0.0 copy-done
  205.4 0.1 convert_element_type.25
  205.6 0.1 convert_element_type.27
  205.7 1.4 fusion
  207.1 1.2 pad_maximum_fusion
  208.3 146.3 %ring_2.1 = (bf16[48,4096]{1,0:T(8,128)(2,1)}, f32[768,256]{1,0:T(8,128)}, f32[768,256]{1,0:T(8,128)}, f32[768,256]{1,0:T(8,128)}) custom-call(bf16[48,4096]{1,0:T(8,128)(2,1)} %get-tuple-element.28.refs_0_, f32[768,256]{1,0:T(8,128)} %bitcast.31, bf16[2,256,4096]{2,1,0:T(8,128)(2,1)} %refs_2_.6, bf16[2,4096]{1,0:T(2,128)(2,1)} %refs_3_.5, ...), custom_call_target="tpu_custom_call" | custom-call | flops 20937965568 | bytes 13958643 | tf_op jit(solution)/shard_map/ring_2/pallas_call | solution.py:372
  354.6 0.0 copy-start.5
  354.6 15.5 %attention.1 = (f32[16,6,8,256]{3,2,1,0:T(8,128)}, bf16[6,2048,256]{2,1,0:T(8,128)(2,1)}, bf16[6,2048,256]{2,1,0:T(8,128)(2,1)}, s32[6,2048]{1,0:T(8,128)}) custom-call(f32[16,6,8,256]{3,2,1,0:T(8,128)} %bitcast.19, f32[16,6,8,256]{3,2,1,0:T(8,128)} %bitcast.20, f32[16,6,8,256]{3,2,1,0:T(8,128)} %bitcast.21, bf16[6,2048,256]{2,1,0:T(8,128)(2,1)} %kc_ref.1, ...), custom_call_target="tpu_custom_call" | custom-call | flops 3221225472 | bytes 25165824 | tf_op jit(solution)/shard_map/attention/pallas_call | solution.py:506
  370.1 0.0 copy-done.5
  370.2 0.6 broadcast_in_dim.4.refs_3_
  370.8 113.7 %ring_3.1 = bf16[48,4096]{1,0:T(8,128)(2,1)} custom-call(bf16[48,4096]{1,0:T(8,128)(2,1)} %get-tuple-element.32.refs_0_, f32[768,256]{1,0:T(8,128)} %bitcast.18, bf16[256,4096]{1,0:T(8,128)(2,1)} %refs_2_.7, bf16[1,4096]{1,0:T(2,128)(2,1)} %broadcast_in_dim.4.refs_3_, bf16[3,4096,768]{2,1,0:T(8,128)(2,1)} %refs_4_.7, bf16[3,4096,768]{2,1,0:T(8,128)(2,1)} %refs_5_.7, ...), custom_call_target="tpu_custom_call" | custom-call | flops 16106127360 | bytes 10737418 | tf_op jit(solution)/shard_map/ring_3/pallas_call | solution.py:372
  484.5 0.0 copy-done.3
  484.5 0.0 copy-done.4
  484.6 0.6 copy.49
  485.2 0.0 copy-done.6
  485.2 0.0 copy-done.7
  485.2 0.6 copy.50
  485.8 1.8 copy.52
  (9 shorter events, 0.1 us)
Async XLA Ops:
  0.6 47.3 %copy-start.1 = (bf16[2,6,3,256]{3,0,2,1:T(2,128)(2,1)S(1)}, bf16[2,6,3,256]{3,0,2,1:T(2,128)(2,1)}, u32[]{:S(2)}) copy-start(bf16[2,6,3,256]{3,0,2,1:T(2,128)(2,1)} %param.34) | copy-start | bytes 55300
  0.6 47.9 %copy-start.2 = (f32[2,6,256]{2,0,1:T(2,128)S(1)}, f32[2,6,256]{2,0,1:T(2,128)}, u32[]{:S(2)}) copy-start(f32[2,6,256]{2,0,1:T(2,128)} %param.35) | copy-start | bytes 36868
  0.7 48.5 %copy-start.8 = (f32[2,256]{1,0:T(2,128)S(1)}, f32[2,256]{1,0:T(2,128)}, u32[]{:S(2)}) copy-start(f32[2,256]{1,0:T(2,128)} %param.50) | copy-start | bytes 6148
  55.0 150.4 %copy-start = (s32[6,128]{1,0:T(8,128)S(1)}, s32[6,128]{1,0:T(8,128)}, u32[]{:S(2)}) copy-start(s32[6,128]{1,0:T(8,128)} %pos_ref.5) | copy-start | bytes 9220
  354.6 15.5 %copy-start.5 = (bf16[4096]{0:T(1024)(128)(2,1)S(1)}, bf16[4096]{0:T(1024)(128)(2,1)}, u32[]{:S(2)}) copy-start(bf16[4096]{0:T(1024)(128)(2,1)} %param.57) | copy-start | bytes 24580
  370.8 113.8 %copy-start.3 = (bf16[6,3,256]{2,1,0:T(4,128)(2,1)S(1)}, bf16[6,3,256]{2,1,0:T(4,128)(2,1)}, u32[]{:S(2)}) copy-start(bf16[6,3,256]{2,1,0:T(4,128)(2,1)} %get-tuple-element.37) | copy-start | bytes 27652
  370.8 113.8 %copy-start.4 = (bf16[6,3,256]{2,1,0:T(4,128)(2,1)S(1)}, bf16[6,3,256]{2,1,0:T(4,128)(2,1)}, u32[]{:S(2)}) copy-start(bf16[6,3,256]{2,1,0:T(4,128)(2,1)} %get-tuple-element.38) | copy-start | bytes 27652
  370.8 114.4 %copy-start.6 = (f32[6,256]{1,0:T(8,128)S(1)}, f32[6,256]{1,0:T(8,128)}, u32[]{:S(2)}) copy-start(f32[6,256]{1,0:T(8,128)} %get-tuple-element.39) | copy-start | bytes 18436
  370.8 114.4 %copy-start.7 = (f32[6,256]{1,0:T(8,128)S(1)}, f32[6,256]{1,0:T(8,128)}, u32[]{:S(2)}) copy-start(f32[6,256]{1,0:T(8,128)} %get-tuple-element.40) | copy-start | bytes 18436

commit v3 on v2

v3 whole, which is shorter than its diff:
```python
import functools

import jax
import jax.numpy as jnp
from jax import lax
from jax.experimental import pallas as pl
from jax.experimental.pallas import tpu as pltpu
from jax.sharding import PartitionSpec as P

WINDOW = 2048
HEAD_DIM = 256
ROPE_DIM = 128
CONV_WIDTH = 4
SCORE_SCALE = 0.0625
NEG_BIG = -1e30
F32 = jnp.float32
BF16 = jnp.bfloat16

SLOT_REL = (0, -1, 1, -2, 2, -3, 3, 4)
ROW_TILE = 16


def slot_of(rel):
    if rel == 0:
        return 0
    if rel in (4, -4):
        return 7
    return -2 * rel - 1 if rel < 0 else 2 * rel


class Net:
    def __init__(self, tp, rows, dim, r):
        self.me = lax.axis_index('tp')
        self.core = lax.rem(self.me, 2)
        self.chips = tp // 2
        self.chip = lax.div(self.me, 2)
        self.up = lax.rem(self.me + 2, tp)
        self.down = lax.rem(self.me + tp - 2, tp)
        self.partner = self.me + 1 - 2 * self.core
        self.rows = rows
        self.groups = rows // ROW_TILE
        self.dim = dim
        self.cw = dim // 2
        self.r = r

    def barrier(self):
        sem = pltpu.get_barrier_semaphore()
        for other in (self.up, self.down, self.partner):
            pl.semaphore_signal(sem, inc=1, device_id={'tp': other}, device_id_type=pl.DeviceIdType.MESH)
        pl.semaphore_wait(sem, 3)

    def span(self, chunk):
        half, group = chunk
        cols = half * self.cw
        if not isinstance(half, int):
            cols = pl.multiple_of(cols, 128)
        return pl.ds(group * ROW_TILE, ROW_TILE), pl.ds(cols, self.cw)

    def remote(self, src, dst, send, recv, dev):
        return pltpu.make_async_remote_copy(src_ref=src, dst_ref=dst, send_sem=send, recv_sem=recv, device_id={'tp': dev}, device_id_type=pl.DeviceIdType.MESH)

    def ag_hop(self, way, d, chunk):
        sign = -1 if way == 0 else 1
        src, dst = slot_of(sign * (d - 1)), slot_of(sign * d)
        g, sems = self.r['g'], (way, d - 1) + chunk
        return self.remote(g.at[(2 * src + self.core,) + self.span(chunk)], g.at[(2 * dst + self.core,) + self.span(chunk)],
                           self.r['send_z'].at[sems], self.r['ag_z'].at[sems], self.up if way == 0 else self.down)

    def ag_pair(self, slot, chunk):
        ref, sems = self.r['g'].at[(2 * slot + self.core,) + self.span(chunk)], (slot,) + chunk
        return self.remote(ref, ref, self.r['send_d'].at[sems], self.r['ag_d'].at[sems], self.partner)

    def rs_pair(self, slot, chunk):
        idx, sems = (slot,) + self.span(chunk), (slot,) + chunk
        return self.remote(self.r['dsend'].at[idx], self.r['drecv'].at[idx], self.r['give_d'].at[sems], self.r['rs_d'].at[sems], self.partner)

    def rs_hop(self, way, d, chunk):
        idx, sems = (way, d - 1) + self.span(chunk), (way, d - 1) + chunk
        return self.remote(self.r['zsend'].at[idx], self.r['zrecv'].at[idx], self.r['give_z'].at[sems], self.r['rs_z'].at[sems], self.up if way == 0 else self.down)

    def chunks(self):
        return [(half, group) for group in range(self.groups) for half in range(2)]

    def hops(self):
        for way in range(2):
            for d in range(1, 5):
                for chunk in self.chunks():
                    if d < 4 or chunk[0] == way:
                        yield way, d, chunk

    def abs_chip(self, rel):
        return lax.rem(self.chip + (rel + self.chips), self.chips)

    def wait_pair(self, slots):
        for slot in slots:
            for chunk in self.chunks():
                self.ag_pair(slot, chunk).wait_recv()

    def gather_start(self, group):
        for k in range(2):
            self.ag_hop(0, 1, (k, group)).start()
            self.ag_hop(1, 1, (1 - k, group)).start()
        for k in range(2):
            self.ag_pair(0, (k, group)).start()

    def gather(self, run_pass):
        for d in range(1, 5):
            for p in range(2 * self.groups if d < 4 else self.groups):
                for way in range(2):
                    chunk = ((p + way) % 2, p // 2) if d < 4 else (way, p)
                    self.ag_hop(way, d, chunk).wait_recv()
                    if d < 3 or (d == 3 and chunk[0] == way):
                        self.ag_hop(way, d + 1, chunk).start()
                    self.ag_pair(slot_of(-d if way == 0 else d), chunk).start()
                if p == 0 and d > 1:
                    first = 0 if d == 2 else 2 * d - 3
                    self.wait_pair(range(first, 2 * d - 1))
                    run_pass(first, 2 * d - 1)

    def gather_end(self, run_pass):
        self.wait_pair((7,))
        run_pass(7, 8)
        for way, d, chunk in self.hops():
            self.ag_hop(way, d, chunk).wait_send()
        for slot in range(8):
            for chunk in self.chunks():
                self.ag_pair(slot, chunk).wait_send()

    def reduce(self, lhs_of, w_ref, finish, between=None):
        r, rows = self.r, self.rows
        sub = min(512, self.cw)
        steps = self.cw // sub

        def slots_of(d):
            return {4: (7,), 0: (0,)}.get(d, (slot_of(-d), slot_of(d)))

        def compute(d):
            slots = slots_of(d)
            for half in range(2):
                def body(t, carry):
                    span = pl.ds(pl.multiple_of(half * self.cw + t * sub, sub), sub)
                    lhs = jnp.concatenate([lhs_of(s, self.core) for s in slots] + [lhs_of(s, 1 - self.core) for s in slots], axis=0)
                    out = jnp.dot(lhs, w_ref[:, span], preferred_element_type=F32)
                    for i, s in enumerate(slots):
                        j = len(slots) + i
                        r['pown'][s, :, span] = out[i * rows:(i + 1) * rows]
                        r['dsend'][s, :, span] = out[j * rows:(j + 1) * rows].astype(BF16)
                    return carry
                lax.fori_loop(0, steps, body, 0)
                for group in range(self.groups):
                    for s in slots:
                        self.rs_pair(s, (half, group)).start()

        def combine(way, d, chunk):
            s = slot_of(d if way == 0 else -d)
            idx = self.span(chunk)
            self.rs_pair(s, chunk).wait_recv()
            total = r['pown'][(s,) + idx] + r['drecv'][(s,) + idx].astype(F32)
            if d < 3 or (d == 3 and chunk[0] == way):
                self.rs_hop(way, d + 1, chunk).wait_recv()
                total = total + r['zrecv'][(way, d) + idx].astype(F32)
            r['zsend'][(way, d - 1) + idx] = total.astype(BF16)
            self.rs_hop(way, d, chunk).start()

        def send(d, deep):
            for group in range(self.groups):
                for way in range(2):
                    combine(way, d, (way if deep else 1 - way, group))

        compute(3)
        send(3, False)
        compute(2)
        if between is not None:
            between()
        compute(4)
        send(2, False)
        send(4, True)
        compute(1)
        send(3, True)
        send(1, False)
        compute(0)
        send(2, True)
        send(1, True)
        for group in range(self.groups):
            for half in range(2):
                self.rs_pair(0, (half, group)).wait_recv()
                self.rs_hop(0, 1, (half, group)).wait_recv()
                self.rs_hop(1, 1, (half, group)).wait_recv()
                idx = self.span((half, group))
                total = r['pown'][(0,) + idx] + r['drecv'][(0,) + idx].astype(F32)
                total = total + r['zrecv'][(0, 0) + idx].astype(F32) + r['zrecv'][(1, 0) + idx].astype(F32)
                finish(idx, total)
            yield group

    def reduce_end(self):
        for way, d, chunk in self.hops():
            self.rs_hop(way, d, chunk).wait_send()
        for slot in range(8):
            for chunk in self.chunks():
                self.rs_pair(slot, chunk).wait_send()


def recurrence(layer, r):
    u_ref, y_ref, pad = r['u'], r['y'], r['pad']
    blocks, seqs, _, width = u_ref.shape
    toks = blocks * 8

    def one_seq(s, carry):
        u = u_ref[:, s].reshape(toks, width)
        pad[8:8 + toks, :] = u
        pad[5:8, :] = r['conv_state'][layer, s].astype(F32)
        r['o_conv'][s] = u[toks - 3:, :].astype(BF16)
        total = jnp.zeros((toks, width), F32)
        for j in range(CONV_WIDTH):
            total = total + pad[5 + j:5 + j + toks, :] * r['conv_w'][layer, j:j + 1, :].astype(F32)
        row_of = lambda key: r[key][layer:layer + 1, :].astype(F32)
        conv = (total + row_of('conv_b')).astype(BF16)
        gate_r = jax.nn.sigmoid(jnp.dot(conv, r['w_a'][layer, 0], preferred_element_type=F32) + row_of('b_a'))
        gate_i = jax.nn.sigmoid(jnp.dot(conv, r['w_i'][layer, 0], preferred_element_type=F32) + row_of('b_i'))
        decay = jnp.exp(-8.0 * gate_r * row_of('soft'))
        reset = r['reset'][s]
        mult = reset + (1.0 - reset) * jnp.sqrt(1.0 - decay * decay)
        decay = decay * (1.0 - reset)
        drive = conv.astype(F32) * gate_i * mult
        a = decay.reshape(blocks, 8, width)
        b = drive.reshape(blocks, 8, width)
        for k in (1, 2, 4):
            inside = r['inside'][k // 2]
            a_sh = pltpu.roll(a, k, 1) * inside + (1.0 - inside)
            b_sh = pltpu.roll(b, k, 1) * inside
            b = a * b_sh + b
            a = a * a_sh
        state = r['lru_state'][layer, pl.ds(s, 1), :]
        for blk in range(blocks):
            h = a[blk] * state + b[blk]
            state = h[7:8, :]
            u_ref[blk, s] = h * y_ref[blk, s]
        r['o_lru'][pl.ds(s, 1), :] = state
        return carry
    lax.fori_loop(0, seqs, one_seq, 0)


def comm_kernel(plan, tp, names, outs, scratch, *refs):
    r = dict(zip(names + outs + scratch, refs))
    x_ref = r['x']
    rows, dim = x_ref.shape
    net = Net(tp, rows, dim, r)
    loads = [[] for _ in plan]
    count = 0
    for i, step in enumerate(plan):
        for key, src, layer in step['loads']:
            view = r[src] if layer is None else r[src].at[layer]
            loads[i].append((key, pltpu.make_async_copy(view, r[key], r['w_sem'].at[count])))
            count += 1
    used = set()
    for step in loads:
        for key, copy in step:
            if key not in used:
                used.add(key)
                copy.start()

    def refill(i):
        for key, _ in loads[i]:
            later = [copy for step in loads[i + 1:] for k, copy in step if k == key]
            if later:
                later[0].start()

    net.barrier()
    xbuf = r['xbuf']
    xbuf[...] = x_ref[...]
    groups = range(net.groups)

    def enter(idx, steps):
        for group in groups if steps is None else steps:
            span = pl.ds(group * ROW_TILE, ROW_TILE)
            h = xbuf[span, :].astype(F32)
            inv = lax.rsqrt(jnp.mean(h * h, axis=-1, keepdims=True) + 1e-6)
            r['g'][net.core, span, :] = (h * inv * (1.0 + r['norm'][idx:idx + 1, :].astype(F32))).astype(BF16)
            net.gather_start(group)
        if steps is not None:
            net.reduce_end()

    def finish_with(bias_ref, idx):
        def finish(span, total):
            xbuf[span] = (xbuf[span].astype(F32) + total + bias_ref[idx:idx + 1, span[1]].astype(F32)).astype(BF16)
        return finish

    def block_of(first, last):
        return r['g'][2 * first:2 * last].reshape((last - first) * 2 * rows, dim)

    def wait_loads(i):
        pending = list(loads[i])

        def wait():
            while pending:
                pending.pop()[1].wait()
        return wait

    reduction = None
    for i, step in enumerate(plan):
        kind, idx = step['kind'], step['idx']
        ready = wait_loads(i)
        if kind == 'pre':
            ready()
            source = r['mid'] if 'mid' in r else r['u']
            r['apre'][...] = source[...].reshape(r['apre'].shape).astype(BF16)

            def lhs_pre(slot, core):
                blk = 2 * net.abs_chip(SLOT_REL[slot]) + core
                return r['apre'][pl.ds(pl.multiple_of(blk * rows, 16), rows), :]
            reduction = net.reduce(lhs_pre, r['w_pre'], finish_with(r['b_pre'], idx))
            owner = i
        elif kind == 'mlp':
            def mlp_pass(first, last, ready=ready, m=idx):
                ready()
                width = 2 * (last - first)

                def body(t, carry):
                    cols = pl.ds(pl.multiple_of(t * 256, 256), 256)
                    lhs = block_of(first, last)
                    h1 = jnp.dot(lhs, r['w_1s'][:, cols], preferred_element_type=F32) + r['b_1'][m:m + 1, cols].astype(F32)
                    h2 = jnp.dot(lhs, r['w_2s'][:, cols], preferred_element_type=F32) + r['b_2'][m:m + 1, cols].astype(F32)
                    act = (jax.nn.gelu(h1, approximate=True) * h2).astype(BF16)
                    r['act'][2 * first:2 * last, :, cols] = act.reshape(width, rows, 256)
                    return carry
                lax.fori_loop(0, r['w_1s'].shape[1] // 256, body, 0)
            enter(2 * idx + 1, reduction)
            refill(owner)
            net.gather(mlp_pass)
            reduction = net.reduce(lambda slot, core: r['act'][2 * slot + core], r['w_ds'], finish_with(r['b_d'], idx), functools.partial(net.gather_end, mlp_pass))
            owner = i
        else:
            def post_pass(first, last, ready=ready, kind=kind, layer=idx):
                ready()
                lhs = block_of(first, last)
                chips = [net.abs_chip(SLOT_REL[s]) for s in range(first, last)]

                def put(ref, value, rope=False):
                    for n, chip in enumerate(chips):
                        v = value[n * 2 * rows:(n + 1) * 2 * rows]
                        if rope:
                            span = pl.ds(pl.multiple_of(chip * 2 * rows, 16), 2 * rows)
                            lo = v[:, :ROPE_DIM]
                            lo = lo * r['cos'][span, :] + pltpu.roll(lo, ROPE_DIM // 2, 1) * r['sin'][span, :]
                            v = jnp.concatenate([lo, v[:, ROPE_DIM:]], axis=1)
                        ref[pl.ds(2 * chip, 2)] = v.astype(BF16).astype(F32).reshape((2,) + ref.shape[1:])
                if kind == 'rec':
                    put(r['u'], jnp.dot(lhs, r['p_0'][...], preferred_element_type=F32) + r['b_x'][layer:layer + 1, :].astype(F32))
                    put(r['y'], jax.nn.gelu(jnp.dot(lhs, r['p_1'][...], preferred_element_type=F32) + r['b_y'][layer:layer + 1, :].astype(F32), approximate=True))
                else:
                    put(r['o_q'], jnp.dot(lhs, r['p_0'][...], preferred_element_type=F32), True)
                    put(r['o_k'], jnp.dot(lhs, r['p_1'][...], preferred_element_type=F32), True)
                    put(r['o_v'], jnp.dot(lhs, r['p_2'][...], preferred_element_type=F32))
            enter(4 if kind == 'attn' else 2 * idx, reduction)
            if reduction is not None:
                refill(owner)
            net.gather(post_pass)
            net.gather_end(post_pass)
            refill(i)
            reduction = None
            if kind == 'rec':
                recurrence(idx, r)
    if reduction is not None:
        for _ in reduction:
            pass
        net.reduce_end()
    r['o_x'][...] = xbuf[...]


def comm_call(tp, ident, x, plan, small, large, outs, extra):
    rows, dim = x.shape
    vmem, hbm = pl.BlockSpec(memory_space=pltpu.VMEM), pl.BlockSpec(memory_space=pl.ANY)
    small = dict(x=x, **small)
    names = list(small) + list(large)
    outs = dict(o_x=jax.ShapeDtypeStruct((rows, dim), BF16), **outs)
    scratch = dict(extra)
    flops = 0
    total = 0
    for step in plan:
        for key, src, layer in step['loads']:
            shape = large[src].shape[-2:]
            scratch.setdefault(key, pltpu.VMEM(shape, BF16))
            flops += 2 * tp * rows * shape[0] * shape[1]
            total += 1
    scratch['pown'] = pltpu.VMEM((8, rows, dim), F32)
    scratch['dsend'] = pltpu.VMEM((8, rows, dim), BF16)
    scratch['drecv'] = pltpu.VMEM((8, rows, dim), BF16)
    scratch['zsend'] = pltpu.VMEM((2, 4, rows, dim), BF16)
    scratch['zrecv'] = pltpu.VMEM((2, 4, rows, dim), BF16)
    scratch['act'] = pltpu.VMEM((tp, rows, scratch['w_1s'].shape[1]), BF16)
    scratch['apre'] = pltpu.VMEM((tp * rows, scratch['w_pre'].shape[0]), BF16)
    scratch['g'] = pltpu.VMEM((tp, rows, dim), BF16)
    scratch['xbuf'] = pltpu.VMEM((rows, dim), BF16)
    for key in ('ag_z', 'rs_z', 'send_z', 'give_z'):
        scratch[key] = pltpu.SemaphoreType.DMA((2, 4, 2, rows // ROW_TILE))
    for key in ('ag_d', 'rs_d', 'send_d', 'give_d'):
        scratch[key] = pltpu.SemaphoreType.DMA((8, 2, rows // ROW_TILE))
    scratch['w_sem'] = pltpu.SemaphoreType.DMA((total,))
    result = pl.pallas_call(
        functools.partial(comm_kernel, plan, tp, names, list(outs), list(scratch)),
        out_shape=tuple(outs.values()),
        in_specs=[vmem] * len(small) + [hbm] * len(large),
        out_specs=tuple(vmem for _ in outs),
        scratch_shapes=list(scratch.values()),
        compiler_params=pltpu.CompilerParams(collective_id=ident, has_side_effects=True, vmem_limit_bytes=67 * 1000 * 1000),
        cost_estimate=pl.CostEstimate(flops=flops, bytes_accessed=flops // 1500, transcendentals=0),
        name='ring_' + str(ident),
    )(*small.values(), *large.values())
    return dict(zip(outs, result))


def attn_kernel(q_ref, k_ref, v_ref, kc_ref, vc_ref, slot_ref, pos_ref, o_ref, ko_ref, vo_ref, so_ref):
    blocks, _, _, width = q_ref.shape
    toks = blocks * 8
    q = (q_ref[...].reshape(toks, width) * SCORE_SCALE).astype(BF16)
    kn = k_ref[...].reshape(toks, width).astype(BF16)
    vn = v_ref[...].reshape(toks, width).astype(BF16)
    kc, vc = kc_ref[0], vc_ref[0]
    seq = pl.ds(pl.program_id(0), 1)
    slot, pos_row = slot_ref[seq, :], pos_ref[seq, :]
    pos_mat = jnp.broadcast_to(pos_row, (toks, toks))
    pos_mat_t = pos_mat.T
    pos_col = pos_mat_t[:, :1]
    row_i = lax.broadcasted_iota(jnp.int32, (toks, toks), 0)
    col_i = lax.broadcasted_iota(jnp.int32, (toks, toks), 1)
    doc_col = jnp.sum(jnp.where((pos_mat == 0) & (col_i <= row_i), 1.0, 0.0), axis=1, keepdims=True)
    doc_row = jnp.sum(jnp.where((pos_mat_t == 0) & (row_i <= col_i), 1.0, 0.0), axis=0, keepdims=True)
    contract = (((1,), (1,)), ((), ()))
    diff_old = jnp.where(doc_col == 0, pos_col, -(2 ** 30)) - jnp.where(slot >= 0, slot, -(2 ** 29))
    keep_old = (diff_old >= 0) & (diff_old < WINDOW)
    diff_new = pos_col - pos_row
    keep_new = (diff_new >= 0) & (diff_new < WINDOW) & (doc_col == doc_row)
    s_old = jnp.where(keep_old, lax.dot_general(q, kc, contract, preferred_element_type=F32), NEG_BIG)
    s_new = jnp.where(keep_new, lax.dot_general(q, kn, contract, preferred_element_type=F32), NEG_BIG)
    top = jnp.maximum(jnp.max(s_old, axis=-1, keepdims=True), jnp.max(s_new, axis=-1, keepdims=True))
    e_old = jnp.exp(s_old - top)
    e_new = jnp.exp(s_new - top)
    denom = jnp.sum(e_old, axis=-1, keepdims=True) + jnp.sum(e_new, axis=-1, keepdims=True)
    inv = 1.0 / denom
    out = jnp.dot((e_old * inv).astype(BF16), vc, preferred_element_type=F32) + jnp.dot((e_new * inv).astype(BF16), vn, preferred_element_type=F32)
    o_ref[...] = out.astype(BF16).astype(F32).reshape(o_ref.shape)
    window = kc.shape[0]
    target_row = lax.rem(pos_row, window)
    target_col = lax.rem(pos_col, window)
    hit = lax.broadcasted_iota(jnp.int32, (window, toks), 0) == target_row
    pick = jnp.where(hit, 1.0, 0.0)
    any_hit = jnp.max(pick, axis=1, keepdims=True) > 0.0
    pick = pick.astype(BF16)
    ko_ref[0] = jnp.where(any_hit, jnp.dot(pick, kn, preferred_element_type=F32), kc.astype(F32)).astype(BF16)
    vo_ref[0] = jnp.where(any_hit, jnp.dot(pick, vn, preferred_element_type=F32), vc.astype(F32)).astype(BF16)
    hit_t = lax.broadcasted_iota(jnp.int32, (toks, window), 1) == target_col
    newest = jnp.max(jnp.where(hit_t, pos_col, -1), axis=0, keepdims=True)
    so_ref[seq, :] = jnp.where(newest >= 0, newest, slot)


def attn_call(q, k, v, k_cache, v_cache, slot_pos, seg_pos):
    seqs, toks = seg_pos.shape
    width = q.shape[-1]
    blocks = toks // 8
    window = k_cache.shape[1]
    shape4 = (blocks, seqs, 8, width)
    tok_spec = pl.BlockSpec((blocks, 1, 8, width), lambda s: (0, s, 0, 0))
    cache_spec = pl.BlockSpec((1, window, width), lambda s: (s, 0, 0))
    row_spec = lambda n: pl.BlockSpec((seqs, n), lambda s: (0, 0))
    out, k_out, v_out, slot_out = pl.pallas_call(
        attn_kernel,
        grid=(seqs,),
        out_shape=(jax.ShapeDtypeStruct(shape4, F32), jax.ShapeDtypeStruct(k_cache.shape, BF16), jax.ShapeDtypeStruct(v_cache.shape, BF16), jax.ShapeDtypeStruct((seqs, window), jnp.int32)),
        in_specs=[tok_spec, tok_spec, tok_spec, cache_spec, cache_spec, row_spec(window), row_spec(toks)],
        out_specs=(tok_spec, cache_spec, cache_spec, row_spec(window)),
        cost_estimate=pl.CostEstimate(flops=8 * seqs * toks * window * width, bytes_accessed=8 * seqs * window * width, transcendentals=0),
        name='attention',
    )(q, k, v, k_cache, v_cache, slot_pos, seg_pos)
    return out, k_out, v_out, slot_out


def solution(mesh):
    tp = mesh.shape['tp']

    def device_body(x_in, seg_pos, conv_state, lru_state, k_cache, v_cache, slot_pos, norm_scale, w_x, b_x, w_y, b_y, conv_w, conv_b, w_a, b_a, w_i, b_i, a_param, w_out, b_out, w_q, w_k, w_v, w_o, b_o, w_1, b_1, w_2, b_2, w_d, b_d):
        seqs, toks = seg_pos.shape
        dim = x_in.shape[-1]
        x = x_in.reshape(-1, dim)
        soft = jax.nn.softplus(a_param)
        half = ROPE_DIM // 2
        timescale = 10000.0 ** (2.0 * jnp.arange(half).astype(F32) / ROPE_DIM)
        order = seg_pos.reshape(seqs, toks // 8, 8).swapaxes(0, 1).reshape(-1)
        angle = order[:, None].astype(F32) / timescale
        sin, cos = jnp.sin(angle), jnp.cos(angle)
        cos2 = jnp.concatenate([cos, cos], axis=1)
        sin2 = jnp.concatenate([-sin, sin], axis=1)

        width = w_q.shape[-1]
        shape4 = (tp, seqs, 8, width)
        tall = jax.ShapeDtypeStruct(shape4, F32)
        inside = (lax.broadcasted_iota(jnp.int32, (3, 8, width), 1) >= jnp.array((1, 2, 4), jnp.int32)[:, None, None]).astype(F32)

        def mlp_step(m):
            return dict(kind='mlp', idx=m, loads=(('w_1s', 'w_1', m), ('w_2s', 'w_2', m), ('w_ds', 'w_d', m)))

        def rec_step(layer):
            return dict(kind='rec', idx=layer, loads=(('p_0', 'w_x', layer), ('p_1', 'w_y', layer)))

        def out_step(layer):
            return dict(kind='pre', idx=layer, loads=(('w_pre', 'w_out', layer),))
        mlp_small = dict(norm=norm_scale, b_1=b_1, b_2=b_2, b_d=b_d)
        mlp_large = dict(w_1=w_1, w_2=w_2, w_d=w_d)
        rec_small = dict(mlp_small, b_pre=b_out, b_x=b_x, b_y=b_y, reset=(seg_pos == 0).astype(F32)[:, :, None], inside=inside, conv_state=conv_state,
                         lru_state=lru_state, conv_w=conv_w, conv_b=conv_b, w_a=w_a, b_a=b_a, w_i=w_i, b_i=b_i, soft=soft)
        rec_large = dict(mlp_large, w_x=w_x, w_y=w_y, w_out=w_out)
        rec_outs = dict(o_conv=jax.ShapeDtypeStruct(conv_state.shape[1:], BF16), o_lru=jax.ShapeDtypeStruct(lru_state.shape[1:], F32))
        work = dict(u=pltpu.VMEM(shape4, F32), y=pltpu.VMEM(shape4, F32), pad=pltpu.VMEM((toks + 8, width), F32))
        zero = comm_call(tp, 0, x, (rec_step(0), out_step(0), mlp_step(0)), rec_small, rec_large, rec_outs, work)
        one = comm_call(
            tp, 1, zero['o_x'],
            (rec_step(1), out_step(1), mlp_step(1), dict(kind='attn', idx=0, loads=(('p_0', 'w_q', None), ('p_1', 'w_k', None), ('p_2', 'w_v', None)))),
            dict(rec_small, cos=cos2, sin=sin2), dict(rec_large, w_q=w_q, w_k=w_k, w_v=w_v), dict(rec_outs, o_q=tall, o_k=tall, o_v=tall), work)
        mid, k_out, v_out, slot_out = attn_call(one['o_q'], one['o_k'], one['o_v'], k_cache, v_cache, slot_pos, seg_pos)
        last = comm_call(
            tp, 2, one['o_x'], (dict(kind='pre', idx=0, loads=(('w_pre', 'w_o', None),)), mlp_step(2)),
            dict(mlp_small, b_pre=b_o[None, :], mid=mid), dict(mlp_large, w_o=w_o), {}, {})
        conv_out = jnp.stack([zero['o_conv'], one['o_conv']])
        lru_out = jnp.stack([zero['o_lru'], one['o_lru']])
        return last['o_x'].reshape(x_in.shape), conv_out, lru_out, k_out, v_out, slot_out

    col_spec = P(None, None, 'tp')
    vec_spec = P(None, 'tp')
    block_spec = P(None, 'tp', None, None)
    row_spec = P(None, 'tp', None)
    cache_spec = P('dp', None, None)
    arg_specs = (P('dp', 'tp', None), P('dp', None), P(None, 'dp', None, 'tp'), P(None, 'dp', 'tp'), cache_spec, cache_spec, P('dp', None), P(), col_spec, vec_spec, col_spec, vec_spec, col_spec, vec_spec, block_spec, vec_spec, block_spec, vec_spec, vec_spec, row_spec, P(), P(None, 'tp'), P(), P(), P('tp', None), P(), col_spec, vec_spec, col_spec, vec_spec, row_spec, P())
    result_specs = (P('dp', 'tp', None), P(None, 'dp', None, 'tp'), P(None, 'dp', 'tp'), cache_spec, cache_spec, P('dp', None))
    return jax.shard_map(device_body, mesh=mesh, in_specs=arg_specs, out_specs=result_specs, check_vma=False)
```

time: 493 us -> 489 us (level)
  Pallas kernels: 479 us -> 467 us
    pallas_call x6 -> x3, Pallas kernels: 463 us -> 452 us  [comm_call(): pl.pallas_call(functools.partial(comm_kernel, plan, tp, names, list(outs)...]
where the time goes in v3:
time: 489 us; the launch traced here: 482 us
  Pallas kernels  467 us (96%)
  local copies, waits for them, and re-layouts  7.41 us (2%)
  other arithmetic  6.62 us (1%)
    pallas_call x3, Pallas kernels, comm_call(): pl.pallas_call(functools.partial(comm_kernel, plan, tp, names, list(outs)...  452 us
    pallas_call x1, Pallas kernels, attn_call(): pl.pallas_call(attn_kernel, grid=(seqs,), out_shape=(jax.ShapeDtypeStruct...  15 us

profile of v3, /device:TPU:21, one launch (start us, length us, event | category | flops | bytes accessed | tf_op | source)
XLA Modules:
  0.0 482.4 jit_solution(2148950880431534268)
XLA Ops:
  0.6 0.7 convert_element_type.29
  1.3 0.1 convert_element_type.30
  1.4 0.1 convert_element_type.32
  1.5 1.4 fusion
  3.0 1.2 pad_maximum_fusion
  4.1 0.7 convert_bitcast_fusion
  4.8 0.9 copy.45.refs_8_
  5.8 1.3 copy.46.refs_10_
  7.1 1.3 fusion.1.refs_9_
  8.4 1.3 copy.47.refs_11_
  9.8 1.3 compare_select_fusion.refs_18_
  11.0 156.4 %ring_0.1 = (bf16[48,4096]{1,0:T(8,128)(2,1)}, bf16[6,3,256]{2,1,0:T(4,128)(2,1)}, f32[6,256]{1,0:T(8,128)}) custom-call(bf16[48,4096]{1,0:T(8,128)(2,1)} %bitcast.15, bf16[6,4096]{1,0:T(8,128)(2,1)} %refs_1_.5, bf16[3,768]{1,0:T(4,128)(2,1)} %refs_2_.5, bf16[3,768]{1,0:T(4,128)(2,1)} %refs_3_.5, bf16[3,4096]{1,0:T(4,128)(2,1)} %refs_4_.5, ...), custom_call_target="tpu_custom_call" | custom-call | flops 19327352832 | bytes 12884901 | tf_op jit(solution)/shard_map/ring_0/pallas_call | solution.py:399
  167.5 182.9 %ring_1.1 = (bf16[48,4096]{1,0:T(8,128)(2,1)}, bf16[6,3,256]{2,1,0:T(4,128)(2,1)}, f32[6,256]{1,0:T(8,128)}, f32[16,6,8,256]{3,2,1,0:T(8,128)}, f32[16,6,8,256]{3,2,1,0:T(8,128)}, /*index=5*/f32[16,6,8,256]{3,2,1,0:T(8,128)}) custom-call(bf16[48,4096]{1,0:T(8,128)(2,1)} %get-tuple-element.19.refs_0_, bf16[6,4096]{1,0:T(8,128)(2,1)} %refs_1_.5, ...), custom_call_target="tpu_custom_call" | custom-call | flops 24159191040 | bytes 16106127 | tf_op jit(solution)/shard_map/ring_1/pallas_call | solution.py:399
  350.4 0.0 copy-start.2
  350.4 15.0 %attention.1 = (f32[16,6,8,256]{3,2,1,0:T(8,128)}, bf16[6,2048,256]{2,1,0:T(8,128)(2,1)}, bf16[6,2048,256]{2,1,0:T(8,128)(2,1)}, s32[6,2048]{1,0:T(8,128)}) custom-call(f32[16,6,8,256]{3,2,1,0:T(8,128)} %get-tuple-element.21.q_ref, f32[16,6,8,256]{3,2,1,0:T(8,128)} %get-tuple-element.22.k_ref, f32[16,6,8,256]{3,2,1,0:T(8,128)} %get-tuple-element.23.v_ref, ...), custom_call_target="tpu_custom_call" | custom-call | flops 3221225472 | bytes 25165824 | tf_op jit(solution)/shard_map/attention/pallas_call | solution.py:465
  365.4 0.0 copy-done.2
  365.4 0.6 broadcast_in_dim.12.refs_5_
  366.0 0.0 copy-start
  366.0 0.0 copy-start.1
  366.0 0.0 copy-start.3
  366.0 0.0 copy-start.4
  366.0 112.9 %ring_2.1 = bf16[48,4096]{1,0:T(8,128)(2,1)} custom-call(bf16[48,4096]{1,0:T(8,128)(2,1)} %get-tuple-element.20.refs_0_, bf16[6,4096]{1,0:T(8,128)(2,1)} %refs_1_.5, bf16[3,768]{1,0:T(4,128)(2,1)} %refs_2_.5, bf16[3,768]{1,0:T(4,128)(2,1)} %refs_3_.5, bf16[3,4096]{1,0:T(4,128)(2,1)} %refs_4_.5, bf16[1,4096]{1,0:T(2,128)(2,1)} %broadcast_in_dim.12.refs_5_, ...), custom_call_target="tpu_custom_call" | custom-call | flops 16106127360 | bytes 10737418 | tf_op jit(solution)/shard_map/ring_2/pallas_call | solution.py:399
  478.9 0.0 copy-done
  479.0 0.0 copy-done.1
  479.0 0.6 copy.52
  479.6 0.0 copy-done.3
  479.6 0.0 copy-done.4
  479.6 0.6 copy.53
  480.2 1.8 copy.55
  (4 shorter events, 0.1 us)
Async XLA Ops:
  350.4 15.0 %copy-start.2 = (bf16[4096]{0:T(1024)(128)(2,1)S(1)}, bf16[4096]{0:T(1024)(128)(2,1)}, u32[]{:S(2)}) copy-start(bf16[4096]{0:T(1024)(128)(2,1)} %param.58) | copy-start | bytes 24580
  366.0 112.9 %copy-start = (bf16[6,3,256]{2,1,0:T(4,128)(2,1)S(1)}, bf16[6,3,256]{2,1,0:T(4,128)(2,1)}, u32[]{:S(2)}) copy-start(bf16[6,3,256]{2,1,0:T(4,128)(2,1)} %get-tuple-element.25) | copy-start | bytes 27652
  366.0 112.9 %copy-start.1 = (bf16[6,3,256]{2,1,0:T(4,128)(2,1)S(1)}, bf16[6,3,256]{2,1,0:T(4,128)(2,1)}, u32[]{:S(2)}) copy-start(bf16[6,3,256]{2,1,0:T(4,128)(2,1)} %get-tuple-element.26) | copy-start | bytes 27652
  366.0 113.6 %copy-start.3 = (f32[6,256]{1,0:T(8,128)S(1)}, f32[6,256]{1,0:T(8,128)}, u32[]{:S(2)}) copy-start(f32[6,256]{1,0:T(8,128)} %get-tuple-element.27) | copy-start | bytes 18436
  366.0 113.6 %copy-start.4 = (f32[6,256]{1,0:T(8,128)S(1)}, f32[6,256]{1,0:T(8,128)}, u32[]{:S(2)}) copy-start(f32[6,256]{1,0:T(8,128)} %get-tuple-element.28) | copy-start | bytes 18436

commit v4 on v3

--- a/solution.py
+++ b/solution.py
@@ -51,10 +51,12 @@
 
     def span(self, chunk):
         half, group = chunk
-        cols = half * self.cw
+        cols, rows = half * self.cw, group * ROW_TILE
         if not isinstance(half, int):
             cols = pl.multiple_of(cols, 128)
-        return pl.ds(group * ROW_TILE, ROW_TILE), pl.ds(cols, self.cw)
+        if not isinstance(group, int):
+            rows = pl.multiple_of(rows, ROW_TILE)
+        return pl.ds(rows, ROW_TILE), pl.ds(cols, self.cw)
 
     def remote(self, src, dst, send, recv, dev):
         return pltpu.make_async_remote_copy(src_ref=src, dst_ref=dst, send_sem=send, recv_sem=recv, device_id={'tp': dev}, device_id_type=pl.DeviceIdType.MESH)
@@ -136,7 +138,8 @@
 
         def compute(d):
             slots = slots_of(d)
-            for half in range(2):
+
+            def one_half(half, outer):
                 def body(t, carry):
                     span = pl.ds(pl.multiple_of(half * self.cw + t * sub, sub), sub)
                     lhs = jnp.concatenate([lhs_of(s, self.core) for s in slots] + [lhs_of(s, 1 - self.core) for s in slots], axis=0)
@@ -150,6 +153,8 @@
                 for group in range(self.groups):
                     for s in slots:
                         self.rs_pair(s, (half, group)).start()
+                return outer
+            lax.fori_loop(0, 2, one_half, 0)
 
         def combine(way, d, chunk):
             s = slot_of(d if way == 0 else -d)
@@ -163,12 +168,15 @@
             self.rs_hop(way, d, chunk).start()
 
         def send(d, deep):
-            for group in range(self.groups):
+            def body(group, carry):
                 for way in range(2):
                     combine(way, d, (way if deep else 1 - way, group))
+                return carry
+            lax.fori_loop(0, self.groups, body, 0)
 
         compute(3)
-        send(3, False)
+        for way in (1, 0):
+            lax.fori_loop(0, self.groups, lambda group, carry, way=way: (combine(way, 3, (1 - way, group)), carry)[1], 0)
         compute(2)
         if between is not None:
             between()
@@ -195,9 +203,17 @@
     def reduce_end(self):
         for way, d, chunk in self.hops():
             self.rs_hop(way, d, chunk).wait_send()
-        for slot in range(8):
+
+        def body(slot, carry):
             for chunk in self.chunks():
                 self.rs_pair(slot, chunk).wait_send()
+            return carry
+        lax.fori_loop(0, 8, body, 0)
+
+
+def column_of(row):
+    n = row.shape[1]
+    return jnp.broadcast_to(row, (n, n)).T[:, :1]
 
 
 def recurrence(layer, r):
@@ -208,7 +224,8 @@
     def one_seq(s, carry):
         u = u_ref[:, s].reshape(toks, width)
         pad[8:8 + toks, :] = u
-        pad[5:8, :] = r['conv_state'][layer, s].astype(F32)
+        for j in range(CONV_WIDTH - 1):
+            pad[5 + j:6 + j, :] = r['conv_state'][s, j].astype(F32)[layer:layer + 1]
         r['o_conv'][s] = u[toks - 3:, :].astype(BF16)
         total = jnp.zeros((toks, width), F32)
         for j in range(CONV_WIDTH):
@@ -218,19 +235,20 @@
         gate_r = jax.nn.sigmoid(jnp.dot(conv, r['w_a'][layer, 0], preferred_element_type=F32) + row_of('b_a'))
         gate_i = jax.nn.sigmoid(jnp.dot(conv, r['w_i'][layer, 0], preferred_element_type=F32) + row_of('b_i'))
         decay = jnp.exp(-8.0 * gate_r * row_of('soft'))
-        reset = r['reset'][s]
-        mult = reset + (1.0 - reset) * jnp.sqrt(1.0 - decay * decay)
-        decay = decay * (1.0 - reset)
+        reset = column_of(r['seg_pos'][pl.ds(s, 1), :]) == 0
+        mult = jnp.where(reset, 1.0, jnp.sqrt(1.0 - decay * decay))
+        decay = jnp.where(reset, 0.0, decay)
         drive = conv.astype(F32) * gate_i * mult
         a = decay.reshape(blocks, 8, width)
         b = drive.reshape(blocks, 8, width)
+        row = lax.broadcasted_iota(jnp.int32, (blocks, 8, width), 1)
         for k in (1, 2, 4):
-            inside = r['inside'][k // 2]
-            a_sh = pltpu.roll(a, k, 1) * inside + (1.0 - inside)
-            b_sh = pltpu.roll(b, k, 1) * inside
+            inside = row >= k
+            a_sh = jnp.where(inside, pltpu.roll(a, k, 1), 1.0)
+            b_sh = jnp.where(inside, pltpu.roll(b, k, 1), 0.0)
             b = a * b_sh + b
             a = a * a_sh
-        state = r['lru_state'][layer, pl.ds(s, 1), :]
+        state = r['lru_state'][s, layer:layer + 1, :]
         for blk in range(blocks):
             h = a[blk] * state + b[blk]
             state = h[7:8, :]
@@ -493,7 +511,6 @@
         width = w_q.shape[-1]
         shape4 = (tp, seqs, 8, width)
         tall = jax.ShapeDtypeStruct(shape4, F32)
-        inside = (lax.broadcasted_iota(jnp.int32, (3, 8, width), 1) >= jnp.array((1, 2, 4), jnp.int32)[:, None, None]).astype(F32)
 
         def mlp_step(m):
             return dict(kind='mlp', idx=m, loads=(('w_1s', 'w_1', m), ('w_2s', 'w_2', m), ('w_ds', 'w_d', m)))
@@ -505,8 +522,8 @@
             return dict(kind='pre', idx=layer, loads=(('w_pre', 'w_out', layer),))
         mlp_small = dict(norm=norm_scale, b_1=b_1, b_2=b_2, b_d=b_d)
         mlp_large = dict(w_1=w_1, w_2=w_2, w_d=w_d)
-        rec_small = dict(mlp_small, b_pre=b_out, b_x=b_x, b_y=b_y, reset=(seg_pos == 0).astype(F32)[:, :, None], inside=inside, conv_state=conv_state,
-                         lru_state=lru_state, conv_w=conv_w, conv_b=conv_b, w_a=w_a, b_a=b_a, w_i=w_i, b_i=b_i, soft=soft)
+        rec_small = dict(mlp_small, b_pre=b_out, b_x=b_x, b_y=b_y, seg_pos=seg_pos, conv_state=conv_state.transpose(1, 2, 0, 3),
+                         lru_state=lru_state.swapaxes(0, 1), conv_w=conv_w, conv_b=conv_b, w_a=w_a, b_a=b_a, w_i=w_i, b_i=b_i, soft=soft)
         rec_large = dict(mlp_large, w_x=w_x, w_y=w_y, w_out=w_out)
         rec_outs = dict(o_conv=jax.ShapeDtypeStruct(conv_state.shape[1:], BF16), o_lru=jax.ShapeDtypeStruct(lru_state.shape[1:], F32))
         work = dict(u=pltpu.VMEM(shape4, F32), y=pltpu.VMEM(shape4, F32), pad=pltpu.VMEM((toks + 8, width), F32))
@@ -519,8 +536,8 @@
         last = comm_call(
             tp, 2, one['o_x'], (dict(kind='pre', idx=0, loads=(('w_pre', 'w_o', None),)), mlp_step(2)),
             dict(mlp_small, b_pre=b_o[None, :], mid=mid), dict(mlp_large, w_o=w_o), {}, {})
-        conv_out = jnp.stack([zero['o_conv'], one['o_conv']])
-        lru_out = jnp.stack([zero['o_lru'], one['o_lru']])
+        conv_out = jnp.stack([zero['o_conv'], one['o_conv']], axis=2).transpose(2, 0, 1, 3)
+        lru_out = jnp.stack([zero['o_lru'], one['o_lru']], axis=1).swapaxes(0, 1)
         return last['o_x'].reshape(x_in.shape), conv_out, lru_out, k_out, v_out, slot_out
 
     col_spec = P(None, None, 'tp')

time: 489 us -> 483 us (0.988)
  no operation moved by 1% of the time
where the time goes in v4:
time: 483 us; the launch traced here: 477 us
  Pallas kernels  467 us (97%)
    pallas_call x3, Pallas kernels, comm_call(): pl.pallas_call(functools.partial(comm_kernel, plan, tp, names, list(outs)...  452 us
    pallas_call x1, Pallas kernels, attn_call(): pl.pallas_call(attn_kernel, grid=(seqs,), out_shape=(jax.ShapeDtypeStruct...  15.2 us

profile of v4, /device:TPU:21, one launch (start us, length us, event | category | flops | bytes accessed | tf_op | source)
XLA Modules:
  0.0 476.9 jit_solution(9319524350163775552)
XLA Ops:
  0.6 0.7 convert_element_type.24
  1.3 0.1 convert_element_type.25
  1.4 0.1 convert_element_type.27
  1.5 1.4 fusion
  3.0 1.2 pad_maximum_fusion
  4.1 1.3 compare_select_fusion.refs_17_
  5.4 156.5 %ring_0.1 = (bf16[48,4096]{1,0:T(8,128)(2,1)}, bf16[6,3,256]{2,1,0:T(4,128)(2,1)}, f32[6,256]{1,0:T(8,128)}) custom-call(bf16[48,4096]{1,0:T(8,128)(2,1)} %bitcast.19, bf16[6,4096]{1,0:T(8,128)(2,1)} %refs_1_.5, bf16[3,768]{1,0:T(4,128)(2,1)} %refs_2_.5, bf16[3,768]{1,0:T(4,128)(2,1)} %refs_3_.5, bf16[3,4096]{1,0:T(4,128)(2,1)} %refs_4_.5, ...), custom_call_target="tpu_custom_call" | custom-call | flops 19327352832 | bytes 12884901 | tf_op jit(solution)/shard_map/ring_0/pallas_call | solution.py:417
  161.9 182.7 %ring_1.1 = (bf16[48,4096]{1,0:T(8,128)(2,1)}, bf16[6,3,256]{2,1,0:T(4,128)(2,1)}, f32[6,256]{1,0:T(8,128)}, f32[16,6,8,256]{3,2,1,0:T(8,128)}, f32[16,6,8,256]{3,2,1,0:T(8,128)}, /*index=5*/f32[16,6,8,256]{3,2,1,0:T(8,128)}) custom-call(bf16[48,4096]{1,0:T(8,128)(2,1)} %get-tuple-element.19.refs_0_, bf16[6,4096]{1,0:T(8,128)(2,1)} %refs_1_.5, ...), custom_call_target="tpu_custom_call" | custom-call | flops 24159191040 | bytes 16106127 | tf_op jit(solution)/shard_map/ring_1/pallas_call | solution.py:417
  344.6 0.0 copy-start.2
  344.7 15.2 %attention.1 = (f32[16,6,8,256]{3,2,1,0:T(8,128)}, bf16[6,2048,256]{2,1,0:T(8,128)(2,1)}, bf16[6,2048,256]{2,1,0:T(8,128)(2,1)}, s32[6,2048]{1,0:T(8,128)}) custom-call(f32[16,6,8,256]{3,2,1,0:T(8,128)} %get-tuple-element.21.q_ref, f32[16,6,8,256]{3,2,1,0:T(8,128)} %get-tuple-element.22.k_ref, f32[16,6,8,256]{3,2,1,0:T(8,128)} %get-tuple-element.23.v_ref, ...), custom_call_target="tpu_custom_call" | custom-call | flops 3221225472 | bytes 25165824 | tf_op jit(solution)/shard_map/attention/pallas_call | solution.py:483
  359.9 0.0 copy-done.2
  359.9 0.6 broadcast_in_dim.4.refs_5_
  360.5 0.0 copy-start
  360.5 0.0 copy-start.1
  360.5 0.0 copy-start.3
  360.5 0.0 copy-start.4
  360.5 112.9 %ring_2.1 = bf16[48,4096]{1,0:T(8,128)(2,1)} custom-call(bf16[48,4096]{1,0:T(8,128)(2,1)} %get-tuple-element.20.refs_0_, bf16[6,4096]{1,0:T(8,128)(2,1)} %refs_1_.5, bf16[3,768]{1,0:T(4,128)(2,1)} %refs_2_.5, bf16[3,768]{1,0:T(4,128)(2,1)} %refs_3_.5, bf16[3,4096]{1,0:T(4,128)(2,1)} %refs_4_.5, bf16[1,4096]{1,0:T(2,128)(2,1)} %broadcast_in_dim.4.refs_5_, ...), custom_call_target="tpu_custom_call" | custom-call | flops 16106127360 | bytes 10737418 | tf_op jit(solution)/shard_map/ring_2/pallas_call | solution.py:417
  473.4 0.0 copy-done
  473.4 0.0 copy-done.1
  473.5 0.6 copy.41
  474.1 0.0 copy-done.3
  474.1 0.0 copy-done.4
  474.1 0.6 copy.42
  474.7 1.8 copy.44
  (4 shorter events, 0.1 us)
Async XLA Ops:
  344.6 15.3 %copy-start.2 = (bf16[4096]{0:T(1024)(128)(2,1)S(1)}, bf16[4096]{0:T(1024)(128)(2,1)}, u32[]{:S(2)}) copy-start(bf16[4096]{0:T(1024)(128)(2,1)} %param.57) | copy-start | bytes 24580
  360.5 112.9 %copy-start = (bf16[6,3,256]{2,1,0:T(4,128)(2,1)S(1)}, bf16[6,3,256]{2,1,0:T(4,128)(2,1)}, u32[]{:S(2)}) copy-start(bf16[6,3,256]{2,1,0:T(4,128)(2,1)} %get-tuple-element.25) | copy-start | bytes 27652
  360.5 112.9 %copy-start.1 = (bf16[6,3,256]{2,1,0:T(4,128)(2,1)S(1)}, bf16[6,3,256]{2,1,0:T(4,128)(2,1)}, u32[]{:S(2)}) copy-start(bf16[6,3,256]{2,1,0:T(4,128)(2,1)} %get-tuple-element.26) | copy-start | bytes 27652
  360.5 113.6 %copy-start.3 = (f32[6,256]{1,0:T(8,128)S(1)}, f32[6,256]{1,0:T(8,128)}, u32[]{:S(2)}) copy-start(f32[6,256]{1,0:T(8,128)} %get-tuple-element.27) | copy-start | bytes 18436
  360.5 113.6 %copy-start.4 = (f32[6,256]{1,0:T(8,128)S(1)}, f32[6,256]{1,0:T(8,128)}, u32[]{:S(2)}) copy-start(f32[6,256]{1,0:T(8,128)} %get-tuple-element.28) | copy-start | bytes 18436

commit v5 on v4

--- a/solution.py
+++ b/solution.py
@@ -43,11 +43,13 @@
         self.cw = dim // 2
         self.r = r
 
-    def barrier(self):
+    def greet(self):
         sem = pltpu.get_barrier_semaphore()
         for other in (self.up, self.down, self.partner):
             pl.semaphore_signal(sem, inc=1, device_id={'tp': other}, device_id_type=pl.DeviceIdType.MESH)
-        pl.semaphore_wait(sem, 3)
+
+    def meet(self):
+        pl.semaphore_wait(pltpu.get_barrier_semaphore(), 3)
 
     def span(self, chunk):
         half, group = chunk
@@ -263,6 +265,7 @@
     x_ref = r['x']
     rows, dim = x_ref.shape
     net = Net(tp, rows, dim, r)
+    net.greet()
     loads = [[] for _ in plan]
     count = 0
     for i, step in enumerate(plan):
@@ -283,19 +286,26 @@
             if later:
                 later[0].start()
 
-    net.barrier()
     xbuf = r['xbuf']
     xbuf[...] = x_ref[...]
     groups = range(net.groups)
 
     def enter(idx, steps):
-        for group in groups if steps is None else steps:
+        def norm(group):
             span = pl.ds(group * ROW_TILE, ROW_TILE)
             h = xbuf[span, :].astype(F32)
             inv = lax.rsqrt(jnp.mean(h * h, axis=-1, keepdims=True) + 1e-6)
             r['g'][net.core, span, :] = (h * inv * (1.0 + r['norm'][idx:idx + 1, :].astype(F32))).astype(BF16)
-            net.gather_start(group)
-        if steps is not None:
+        if steps is None:
+            for group in groups:
+                norm(group)
+            net.meet()
+            for group in groups:
+                net.gather_start(group)
+        else:
+            for group in steps:
+                norm(group)
+                net.gather_start(group)
             net.reduce_end()
 
     def finish_with(bias_ref, idx):
@@ -322,6 +332,8 @@
             ready()
             source = r['mid'] if 'mid' in r else r['u']
             r['apre'][...] = source[...].reshape(r['apre'].shape).astype(BF16)
+            if i == 0:
+                net.meet()
 
             def lhs_pre(slot, core):
                 blk = 2 * net.abs_chip(SLOT_REL[slot]) + core

time: 483 us -> 482 us (level)
  no operation moved by 1% of the time
where the time goes in v5:
time: 482 us; the launch traced here: 476 us
  Pallas kernels  467 us (97%)
    pallas_call x3, Pallas kernels, comm_call(): pl.pallas_call(functools.partial(comm_kernel, plan, tp, names, list(outs)...  452 us
    pallas_call x1, Pallas kernels, attn_call(): pl.pallas_call(attn_kernel, grid=(seqs,), out_shape=(jax.ShapeDtypeStruct...  15.2 us

profile of v5, /device:TPU:21, one launch (start us, length us, event | category | flops | bytes accessed | tf_op | source)
XLA Modules:
  0.0 476.4 jit_solution(15323985763607326859)
XLA Ops:
  0.6 0.7 convert_element_type.24
  1.3 0.1 convert_element_type.25
  1.4 0.1 convert_element_type.27
  1.5 1.4 fusion
  3.0 1.2 pad_maximum_fusion
  4.1 1.3 compare_select_fusion.refs_17_
  5.4 156.3 %ring_0.1 = (bf16[48,4096]{1,0:T(8,128)(2,1)}, bf16[6,3,256]{2,1,0:T(4,128)(2,1)}, f32[6,256]{1,0:T(8,128)}) custom-call(bf16[48,4096]{1,0:T(8,128)(2,1)} %bitcast.19, bf16[6,4096]{1,0:T(8,128)(2,1)} %refs_1_.5, bf16[3,768]{1,0:T(4,128)(2,1)} %refs_2_.5, bf16[3,768]{1,0:T(4,128)(2,1)} %refs_3_.5, bf16[3,4096]{1,0:T(4,128)(2,1)} %refs_4_.5, ...), custom_call_target="tpu_custom_call" | custom-call | flops 19327352832 | bytes 12884901 | tf_op jit(solution)/shard_map/ring_0/pallas_call | solution.py:429
  161.7 182.5 %ring_1.1 = (bf16[48,4096]{1,0:T(8,128)(2,1)}, bf16[6,3,256]{2,1,0:T(4,128)(2,1)}, f32[6,256]{1,0:T(8,128)}, f32[16,6,8,256]{3,2,1,0:T(8,128)}, f32[16,6,8,256]{3,2,1,0:T(8,128)}, /*index=5*/f32[16,6,8,256]{3,2,1,0:T(8,128)}) custom-call(bf16[48,4096]{1,0:T(8,128)(2,1)} %get-tuple-element.19.refs_0_, bf16[6,4096]{1,0:T(8,128)(2,1)} %refs_1_.5, ...), custom_call_target="tpu_custom_call" | custom-call | flops 24159191040 | bytes 16106127 | tf_op jit(solution)/shard_map/ring_1/pallas_call | solution.py:429
  344.3 0.0 copy-start.2
  344.3 15.2 %attention.1 = (f32[16,6,8,256]{3,2,1,0:T(8,128)}, bf16[6,2048,256]{2,1,0:T(8,128)(2,1)}, bf16[6,2048,256]{2,1,0:T(8,128)(2,1)}, s32[6,2048]{1,0:T(8,128)}) custom-call(f32[16,6,8,256]{3,2,1,0:T(8,128)} %get-tuple-element.21.q_ref, f32[16,6,8,256]{3,2,1,0:T(8,128)} %get-tuple-element.22.k_ref, f32[16,6,8,256]{3,2,1,0:T(8,128)} %get-tuple-element.23.v_ref, ...), custom_call_target="tpu_custom_call" | custom-call | flops 3221225472 | bytes 25165824 | tf_op jit(solution)/shard_map/attention/pallas_call | solution.py:495
  359.5 0.0 copy-done.2
  359.5 0.6 broadcast_in_dim.4.refs_5_
  360.2 0.0 copy-start
  360.2 0.0 copy-start.1
  360.2 0.0 copy-start.3
  360.2 0.0 copy-start.4
  360.2 112.8 %ring_2.1 = bf16[48,4096]{1,0:T(8,128)(2,1)} custom-call(bf16[48,4096]{1,0:T(8,128)(2,1)} %get-tuple-element.20.refs_0_, bf16[6,4096]{1,0:T(8,128)(2,1)} %refs_1_.5, bf16[3,768]{1,0:T(4,128)(2,1)} %refs_2_.5, bf16[3,768]{1,0:T(4,128)(2,1)} %refs_3_.5, bf16[3,4096]{1,0:T(4,128)(2,1)} %refs_4_.5, bf16[1,4096]{1,0:T(2,128)(2,1)} %broadcast_in_dim.4.refs_5_, ...), custom_call_target="tpu_custom_call" | custom-call | flops 16106127360 | bytes 10737418 | tf_op jit(solution)/shard_map/ring_2/pallas_call | solution.py:429
  472.9 0.0 copy-done
  473.0 0.0 copy-done.1
  473.0 0.6 copy.41
  473.6 0.0 copy-done.3
  473.6 0.0 copy-done.4
  473.6 0.6 copy.42
  474.2 1.8 copy.44
  (4 shorter events, 0.1 us)
Async XLA Ops:
  344.3 15.3 %copy-start.2 = (bf16[4096]{0:T(1024)(128)(2,1)S(1)}, bf16[4096]{0:T(1024)(128)(2,1)}, u32[]{:S(2)}) copy-start(bf16[4096]{0:T(1024)(128)(2,1)} %param.57) | copy-start | bytes 24580
  360.2 112.8 %copy-start = (bf16[6,3,256]{2,1,0:T(4,128)(2,1)S(1)}, bf16[6,3,256]{2,1,0:T(4,128)(2,1)}, u32[]{:S(2)}) copy-start(bf16[6,3,256]{2,1,0:T(4,128)(2,1)} %get-tuple-element.25) | copy-start | bytes 27652
  360.2 112.8 %copy-start.1 = (bf16[6,3,256]{2,1,0:T(4,128)(2,1)S(1)}, bf16[6,3,256]{2,1,0:T(4,128)(2,1)}, u32[]{:S(2)}) copy-start(bf16[6,3,256]{2,1,0:T(4,128)(2,1)} %get-tuple-element.26) | copy-start | bytes 27652
  360.2 113.5 %copy-start.3 = (f32[6,256]{1,0:T(8,128)S(1)}, f32[6,256]{1,0:T(8,128)}, u32[]{:S(2)}) copy-start(f32[6,256]{1,0:T(8,128)} %get-tuple-element.27) | copy-start | bytes 18436
  360.2 113.5 %copy-start.4 = (f32[6,256]{1,0:T(8,128)S(1)}, f32[6,256]{1,0:T(8,128)}, u32[]{:S(2)}) copy-start(f32[6,256]{1,0:T(8,128)} %get-tuple-element.28) | copy-start | bytes 18436
